TPU v7x, 8 devices: a whole 2x2x1 slice. The times are simulated.
8 devices in a mesh: row: 4 (over z, y, x), col: 2 (over core).
Axes of the slice: x: 2, y: 2, z: 1, core: 2. Of those that a mesh axis runs over, the one named last changes fastest.
Arguments:
- v_panels: float32 [4096, 4096], P('row', 'col')
- t_factors: float32 [64, 64, 64], P('col')
- z_vecs: float32 [4096, 4096], P(None, ('row', 'col'))
Outputs:
- output: float32 [4096, 4096], P(None, ('row', 'col'))
All inputs are finite; a program needn't handle non-finite values.
Results may differ from a plain program's by a relative error of at most 0.001.
Values sent between devices are 32-bit elements.
A program may use at most 1 GiB of HBM per device.

v0:
```python
import jax
import jax.numpy as jnp
from jax import lax
from jax.sharding import PartitionSpec as P, NamedSharding

FULL_PREC = lax.Precision.HIGHEST
CONTRACT_ROWS = (((0,), (0,)), ((), ()))


def solution(mesh):
    col_dev = mesh.shape["col"]

    def local_apply(v_loc, t_loc, z_loc):
        num_local = t_loc.shape[0]
        block_w = t_loc.shape[1]
        x_two = lax.all_to_all(z_loc, "row", 0, 1, tiled=True)

        def outer_step(step_idx, x_cur):
            local_idx = num_local - 1 - step_idx
            v_own = lax.dynamic_slice_in_dim(v_loc, local_idx * block_w, block_w, axis=1)
            t_own = lax.dynamic_index_in_dim(t_loc, local_idx, axis=0, keepdims=False)
            v_all = lax.all_gather(v_own, "col")
            t_all = lax.all_gather(t_own, "col")

            def inner_step(sub_idx, x_in):
                owner_col = col_dev - 1 - sub_idx
                v_blk = v_all[owner_col]
                t_blk = t_all[owner_col]
                w_part = lax.dot_general(v_blk, x_in, CONTRACT_ROWS, precision=FULL_PREC, preferred_element_type=jnp.float32)
                w_sum = lax.psum(w_part, "row")
                y_blk = jnp.dot(t_blk, w_sum, precision=FULL_PREC, preferred_element_type=jnp.float32)
                return x_in - jnp.dot(v_blk, y_blk, precision=FULL_PREC, preferred_element_type=jnp.float32)

            return lax.fori_loop(0, col_dev, inner_step, x_cur)

        x_two = lax.fori_loop(0, num_local, outer_step, x_two)
        return lax.all_to_all(x_two, "row", 1, 0, tiled=True)

    return jax.shard_map(
        local_apply,
        mesh=mesh,
        in_specs=(P("row", "col"), P("col", None, None), P(None, ("row", "col"))),
        out_specs=P(None, ("row", "col")),
        check_vma=False,
    )
```

profile of v0, /device:TPU:0, one launch (start us, length us, event | category | flops | bytes accessed | tf_op | source)
XLA Modules:
  0.0 3935.4 jit_solution(7064593209843589918)
XLA Ops:
  12.2 94.0 %all-to-all-done = f32[4,1024,512]{2,1,0:T(8,128)} async-done(((f32[4,1024,512]{2,1,0:T(8,128)}), f32[4,1024,512]{2,1,0:T(8,128)}, u32[]{:S(2)}, u32[]{:S(2)}) %all-to-all-start) | async-done | bytes 8388640 | tf_op jit(solution)/shard_map/all_to_all | solution.py:16
  124.1 3701.2 %while.44 = (s32[]{:T(128)}, f32[1024,2048]{1,0:T(8,128)}, f32[1024,2048]{1,0:T(8,128)}, f32[32,64,64]{2,1,0:T(8,128)}, s32[]{:T(128)}, /*index=5*/s32[]{:T(128)...) while((s32[]{:T(128)}, f32[1024,2048]{1,0:T(8,128)}, ...), condition=%wide.region_4.5_spmd, body=%wide.region_0.4_spmd.sunk | while | flops 3324116992 | bytes 32883160 | solution.py:36
  130.5 109.4 %while.45 = (s32[]{:T(128)}, f32[1024,2048]{1,0:T(8,128)}, f32[2,1024,64]{2,1,0:T(8,128)S(1)}, f32[2,64,64]{2,1,0:T(8,128)S(1)}, s32[]{:T(128)}, /*index=5*/s32[]{:T(128)}, s32[]{:T(128)}) while((s32[]{:T(128)}, f32[1024,2048]{1,0:T(8,128)}, f32[2,1024,64]{2,1,0:T(8,128)S(1)}, f32[2,64,64]{2,1,0:T(8,128)S(1)}, s32[]{:T(128)}, ...), condition=%wide.region_3.3_spmd, body=%wide.region_1.2_spmd.sunk | while | flops 3324116992 | bytes 31490224 | solution.py:34
  138.8 34.0 all-reduce.2.cloned.1.call-done
  193.6 33.9 all-reduce.2.cloned.1.call-done
  246.3 109.2 %while.45 = (s32[]{:T(128)}, f32[1024,2048]{1,0:T(8,128)}, f32[2,1024,64]{2,1,0:T(8,128)S(1)}, f32[2,64,64]{2,1,0:T(8,128)S(1)}, s32[]{:T(128)}, /*index=5*/s32[]{:T(128)}, s32[]{:T(128)}) while((s32[]{:T(128)}, f32[1024,2048]{1,0:T(8,128)}, f32[2,1024,64]{2,1,0:T(8,128)S(1)}, f32[2,64,64]{2,1,0:T(8,128)S(1)}, s32[]{:T(128)}, ...), condition=%wide.region_3.3_spmd, body=%wide.region_1.2_spmd.sunk | while | flops 3324116992 | bytes 31490224 | solution.py:34
  362.0 109.3 %while.45 = (s32[]{:T(128)}, f32[1024,2048]{1,0:T(8,128)}, f32[2,1024,64]{2,1,0:T(8,128)S(1)}, f32[2,64,64]{2,1,0:T(8,128)S(1)}, s32[]{:T(128)}, /*index=5*/s32[]{:T(128)}, s32[]{:T(128)}) while((s32[]{:T(128)}, f32[1024,2048]{1,0:T(8,128)}, f32[2,1024,64]{2,1,0:T(8,128)S(1)}, f32[2,64,64]{2,1,0:T(8,128)S(1)}, s32[]{:T(128)}, ...), condition=%wide.region_3.3_spmd, body=%wide.region_1.2_spmd.sunk | while | flops 3324116992 | bytes 31490224 | solution.py:34
  370.3 33.9 all-reduce.2.cloned.1.call-done
  424.9 33.9 all-reduce.2.cloned.1.call-done
  477.6 109.2 %while.45 = (s32[]{:T(128)}, f32[1024,2048]{1,0:T(8,128)}, f32[2,1024,64]{2,1,0:T(8,128)S(1)}, f32[2,64,64]{2,1,0:T(8,128)S(1)}, s32[]{:T(128)}, /*index=5*/s32[]{:T(128)}, s32[]{:T(128)}) while((s32[]{:T(128)}, f32[1024,2048]{1,0:T(8,128)}, f32[2,1024,64]{2,1,0:T(8,128)S(1)}, f32[2,64,64]{2,1,0:T(8,128)S(1)}, s32[]{:T(128)}, ...), condition=%wide.region_3.3_spmd, body=%wide.region_1.2_spmd.sunk | while | flops 3324116992 | bytes 31490224 | solution.py:34
  593.3 109.3 %while.45 = (s32[]{:T(128)}, f32[1024,2048]{1,0:T(8,128)}, f32[2,1024,64]{2,1,0:T(8,128)S(1)}, f32[2,64,64]{2,1,0:T(8,128)S(1)}, s32[]{:T(128)}, /*index=5*/s32[]{:T(128)}, s32[]{:T(128)}) while((s32[]{:T(128)}, f32[1024,2048]{1,0:T(8,128)}, f32[2,1024,64]{2,1,0:T(8,128)S(1)}, f32[2,64,64]{2,1,0:T(8,128)S(1)}, s32[]{:T(128)}, ...), condition=%wide.region_3.3_spmd, body=%wide.region_1.2_spmd.sunk | while | flops 3324116992 | bytes 31490224 | solution.py:34
  601.6 33.9 all-reduce.2.cloned.1.call-done
  656.2 33.9 all-reduce.2.cloned.1.call-done
  708.9 109.2 %while.45 = (s32[]{:T(128)}, f32[1024,2048]{1,0:T(8,128)}, f32[2,1024,64]{2,1,0:T(8,128)S(1)}, f32[2,64,64]{2,1,0:T(8,128)S(1)}, s32[]{:T(128)}, /*index=5*/s32[]{:T(128)}, s32[]{:T(128)}) while((s32[]{:T(128)}, f32[1024,2048]{1,0:T(8,128)}, f32[2,1024,64]{2,1,0:T(8,128)S(1)}, f32[2,64,64]{2,1,0:T(8,128)S(1)}, s32[]{:T(128)}, ...), condition=%wide.region_3.3_spmd, body=%wide.region_1.2_spmd.sunk | while | flops 3324116992 | bytes 31490224 | solution.py:34
  824.6 109.3 %while.45 = (s32[]{:T(128)}, f32[1024,2048]{1,0:T(8,128)}, f32[2,1024,64]{2,1,0:T(8,128)S(1)}, f32[2,64,64]{2,1,0:T(8,128)S(1)}, s32[]{:T(128)}, /*index=5*/s32[]{:T(128)}, s32[]{:T(128)}) while((s32[]{:T(128)}, f32[1024,2048]{1,0:T(8,128)}, f32[2,1024,64]{2,1,0:T(8,128)S(1)}, f32[2,64,64]{2,1,0:T(8,128)S(1)}, s32[]{:T(128)}, ...), condition=%wide.region_3.3_spmd, body=%wide.region_1.2_spmd.sunk | while | flops 3324116992 | bytes 31490224 | solution.py:34
  832.9 33.9 all-reduce.2.cloned.1.call-done
  887.5 33.9 all-reduce.2.cloned.1.call-done
  940.2 109.2 %while.45 = (s32[]{:T(128)}, f32[1024,2048]{1,0:T(8,128)}, f32[2,1024,64]{2,1,0:T(8,128)S(1)}, f32[2,64,64]{2,1,0:T(8,128)S(1)}, s32[]{:T(128)}, /*index=5*/s32[]{:T(128)}, s32[]{:T(128)}) while((s32[]{:T(128)}, f32[1024,2048]{1,0:T(8,128)}, f32[2,1024,64]{2,1,0:T(8,128)S(1)}, f32[2,64,64]{2,1,0:T(8,128)S(1)}, s32[]{:T(128)}, ...), condition=%wide.region_3.3_spmd, body=%wide.region_1.2_spmd.sunk | while | flops 3324116992 | bytes 31490224 | solution.py:34
  1055.9 109.3 %while.45 = (s32[]{:T(128)}, f32[1024,2048]{1,0:T(8,128)}, f32[2,1024,64]{2,1,0:T(8,128)S(1)}, f32[2,64,64]{2,1,0:T(8,128)S(1)}, s32[]{:T(128)}, /*index=5*/s32[]{:T(128)}, s32[]{:T(128)}) while((s32[]{:T(128)}, f32[1024,2048]{1,0:T(8,128)}, f32[2,1024,64]{2,1,0:T(8,128)S(1)}, f32[2,64,64]{2,1,0:T(8,128)S(1)}, s32[]{:T(128)}, ...), condition=%wide.region_3.3_spmd, body=%wide.region_1.2_spmd.sunk | while | flops 3324116992 | bytes 31490224 | solution.py:34
  1064.2 33.9 all-reduce.2.cloned.1.call-done
  1118.8 33.9 all-reduce.2.cloned.1.call-done
  1171.6 109.2 %while.45 = (s32[]{:T(128)}, f32[1024,2048]{1,0:T(8,128)}, f32[2,1024,64]{2,1,0:T(8,128)S(1)}, f32[2,64,64]{2,1,0:T(8,128)S(1)}, s32[]{:T(128)}, /*index=5*/s32[]{:T(128)}, s32[]{:T(128)}) while((s32[]{:T(128)}, f32[1024,2048]{1,0:T(8,128)}, f32[2,1024,64]{2,1,0:T(8,128)S(1)}, f32[2,64,64]{2,1,0:T(8,128)S(1)}, s32[]{:T(128)}, ...), condition=%wide.region_3.3_spmd, body=%wide.region_1.2_spmd.sunk | while | flops 3324116992 | bytes 31490224 | solution.py:34
  1287.2 109.3 %while.45 = (s32[]{:T(128)}, f32[1024,2048]{1,0:T(8,128)}, f32[2,1024,64]{2,1,0:T(8,128)S(1)}, f32[2,64,64]{2,1,0:T(8,128)S(1)}, s32[]{:T(128)}, /*index=5*/s32[]{:T(128)}, s32[]{:T(128)}) while((s32[]{:T(128)}, f32[1024,2048]{1,0:T(8,128)}, f32[2,1024,64]{2,1,0:T(8,128)S(1)}, f32[2,64,64]{2,1,0:T(8,128)S(1)}, s32[]{:T(128)}, ...), condition=%wide.region_3.3_spmd, body=%wide.region_1.2_spmd.sunk | while | flops 3324116992 | bytes 31490224 | solution.py:34
  1295.5 33.9 all-reduce.2.cloned.1.call-done
  1350.2 33.9 all-reduce.2.cloned.1.call-done
  1402.9 109.2 %while.45 = (s32[]{:T(128)}, f32[1024,2048]{1,0:T(8,128)}, f32[2,1024,64]{2,1,0:T(8,128)S(1)}, f32[2,64,64]{2,1,0:T(8,128)S(1)}, s32[]{:T(128)}, /*index=5*/s32[]{:T(128)}, s32[]{:T(128)}) while((s32[]{:T(128)}, f32[1024,2048]{1,0:T(8,128)}, f32[2,1024,64]{2,1,0:T(8,128)S(1)}, f32[2,64,64]{2,1,0:T(8,128)S(1)}, s32[]{:T(128)}, ...), condition=%wide.region_3.3_spmd, body=%wide.region_1.2_spmd.sunk | while | flops 3324116992 | bytes 31490224 | solution.py:34
  1518.5 109.3 %while.45 = (s32[]{:T(128)}, f32[1024,2048]{1,0:T(8,128)}, f32[2,1024,64]{2,1,0:T(8,128)S(1)}, f32[2,64,64]{2,1,0:T(8,128)S(1)}, s32[]{:T(128)}, /*index=5*/s32[]{:T(128)}, s32[]{:T(128)}) while((s32[]{:T(128)}, f32[1024,2048]{1,0:T(8,128)}, f32[2,1024,64]{2,1,0:T(8,128)S(1)}, f32[2,64,64]{2,1,0:T(8,128)S(1)}, s32[]{:T(128)}, ...), condition=%wide.region_3.3_spmd, body=%wide.region_1.2_spmd.sunk | while | flops 3324116992 | bytes 31490224 | solution.py:34
  1526.9 33.9 all-reduce.2.cloned.1.call-done
  1581.5 33.9 all-reduce.2.cloned.1.call-done
  1634.2 109.2 %while.45 = (s32[]{:T(128)}, f32[1024,2048]{1,0:T(8,128)}, f32[2,1024,64]{2,1,0:T(8,128)S(1)}, f32[2,64,64]{2,1,0:T(8,128)S(1)}, s32[]{:T(128)}, /*index=5*/s32[]{:T(128)}, s32[]{:T(128)}) while((s32[]{:T(128)}, f32[1024,2048]{1,0:T(8,128)}, f32[2,1024,64]{2,1,0:T(8,128)S(1)}, f32[2,64,64]{2,1,0:T(8,128)S(1)}, s32[]{:T(128)}, ...), condition=%wide.region_3.3_spmd, body=%wide.region_1.2_spmd.sunk | while | flops 3324116992 | bytes 31490224 | solution.py:34
  1749.9 109.3 %while.45 = (s32[]{:T(128)}, f32[1024,2048]{1,0:T(8,128)}, f32[2,1024,64]{2,1,0:T(8,128)S(1)}, f32[2,64,64]{2,1,0:T(8,128)S(1)}, s32[]{:T(128)}, /*index=5*/s32[]{:T(128)}, s32[]{:T(128)}) while((s32[]{:T(128)}, f32[1024,2048]{1,0:T(8,128)}, f32[2,1024,64]{2,1,0:T(8,128)S(1)}, f32[2,64,64]{2,1,0:T(8,128)S(1)}, s32[]{:T(128)}, ...), condition=%wide.region_3.3_spmd, body=%wide.region_1.2_spmd.sunk | while | flops 3324116992 | bytes 31490224 | solution.py:34
  1758.2 33.9 all-reduce.2.cloned.1.call-done
  1812.8 33.9 all-reduce.2.cloned.1.call-done
  1865.5 109.2 %while.45 = (s32[]{:T(128)}, f32[1024,2048]{1,0:T(8,128)}, f32[2,1024,64]{2,1,0:T(8,128)S(1)}, f32[2,64,64]{2,1,0:T(8,128)S(1)}, s32[]{:T(128)}, /*index=5*/s32[]{:T(128)}, s32[]{:T(128)}) while((s32[]{:T(128)}, f32[1024,2048]{1,0:T(8,128)}, f32[2,1024,64]{2,1,0:T(8,128)S(1)}, f32[2,64,64]{2,1,0:T(8,128)S(1)}, s32[]{:T(128)}, ...), condition=%wide.region_3.3_spmd, body=%wide.region_1.2_spmd.sunk | while | flops 3324116992 | bytes 31490224 | solution.py:34
  1981.2 109.3 %while.45 = (s32[]{:T(128)}, f32[1024,2048]{1,0:T(8,128)}, f32[2,1024,64]{2,1,0:T(8,128)S(1)}, f32[2,64,64]{2,1,0:T(8,128)S(1)}, s32[]{:T(128)}, /*index=5*/s32[]{:T(128)}, s32[]{:T(128)}) while((s32[]{:T(128)}, f32[1024,2048]{1,0:T(8,128)}, f32[2,1024,64]{2,1,0:T(8,128)S(1)}, f32[2,64,64]{2,1,0:T(8,128)S(1)}, s32[]{:T(128)}, ...), condition=%wide.region_3.3_spmd, body=%wide.region_1.2_spmd.sunk | while | flops 3324116992 | bytes 31490224 | solution.py:34
  1989.5 33.9 all-reduce.2.cloned.1.call-done
  2044.1 33.9 all-reduce.2.cloned.1.call-done
  2096.8 109.2 %while.45 = (s32[]{:T(128)}, f32[1024,2048]{1,0:T(8,128)}, f32[2,1024,64]{2,1,0:T(8,128)S(1)}, f32[2,64,64]{2,1,0:T(8,128)S(1)}, s32[]{:T(128)}, /*index=5*/s32[]{:T(128)}, s32[]{:T(128)}) while((s32[]{:T(128)}, f32[1024,2048]{1,0:T(8,128)}, f32[2,1024,64]{2,1,0:T(8,128)S(1)}, f32[2,64,64]{2,1,0:T(8,128)S(1)}, s32[]{:T(128)}, ...), condition=%wide.region_3.3_spmd, body=%wide.region_1.2_spmd.sunk | while | flops 3324116992 | bytes 31490224 | solution.py:34
  2212.5 109.3 %while.45 = (s32[]{:T(128)}, f32[1024,2048]{1,0:T(8,128)}, f32[2,1024,64]{2,1,0:T(8,128)S(1)}, f32[2,64,64]{2,1,0:T(8,128)S(1)}, s32[]{:T(128)}, /*index=5*/s32[]{:T(128)}, s32[]{:T(128)}) while((s32[]{:T(128)}, f32[1024,2048]{1,0:T(8,128)}, f32[2,1024,64]{2,1,0:T(8,128)S(1)}, f32[2,64,64]{2,1,0:T(8,128)S(1)}, s32[]{:T(128)}, ...), condition=%wide.region_3.3_spmd, body=%wide.region_1.2_spmd.sunk | while | flops 3324116992 | bytes 31490224 | solution.py:34
  2220.8 33.9 all-reduce.2.cloned.1.call-done
  2275.4 33.9 all-reduce.2.cloned.1.call-done
  2328.2 109.2 %while.45 = (s32[]{:T(128)}, f32[1024,2048]{1,0:T(8,128)}, f32[2,1024,64]{2,1,0:T(8,128)S(1)}, f32[2,64,64]{2,1,0:T(8,128)S(1)}, s32[]{:T(128)}, /*index=5*/s32[]{:T(128)}, s32[]{:T(128)}) while((s32[]{:T(128)}, f32[1024,2048]{1,0:T(8,128)}, f32[2,1024,64]{2,1,0:T(8,128)S(1)}, f32[2,64,64]{2,1,0:T(8,128)S(1)}, s32[]{:T(128)}, ...), condition=%wide.region_3.3_spmd, body=%wide.region_1.2_spmd.sunk | while | flops 3324116992 | bytes 31490224 | solution.py:34
  2443.8 109.3 %while.45 = (s32[]{:T(128)}, f32[1024,2048]{1,0:T(8,128)}, f32[2,1024,64]{2,1,0:T(8,128)S(1)}, f32[2,64,64]{2,1,0:T(8,128)S(1)}, s32[]{:T(128)}, /*index=5*/s32[]{:T(128)}, s32[]{:T(128)}) while((s32[]{:T(128)}, f32[1024,2048]{1,0:T(8,128)}, f32[2,1024,64]{2,1,0:T(8,128)S(1)}, f32[2,64,64]{2,1,0:T(8,128)S(1)}, s32[]{:T(128)}, ...), condition=%wide.region_3.3_spmd, body=%wide.region_1.2_spmd.sunk | while | flops 3324116992 | bytes 31490224 | solution.py:34
  2452.1 33.9 all-reduce.2.cloned.1.call-done
  2506.8 33.9 all-reduce.2.cloned.1.call-done
  2559.5 109.2 %while.45 = (s32[]{:T(128)}, f32[1024,2048]{1,0:T(8,128)}, f32[2,1024,64]{2,1,0:T(8,128)S(1)}, f32[2,64,64]{2,1,0:T(8,128)S(1)}, s32[]{:T(128)}, /*index=5*/s32[]{:T(128)}, s32[]{:T(128)}) while((s32[]{:T(128)}, f32[1024,2048]{1,0:T(8,128)}, f32[2,1024,64]{2,1,0:T(8,128)S(1)}, f32[2,64,64]{2,1,0:T(8,128)S(1)}, s32[]{:T(128)}, ...), condition=%wide.region_3.3_spmd, body=%wide.region_1.2_spmd.sunk | while | flops 3324116992 | bytes 31490224 | solution.py:34
  2675.1 109.3 %while.45 = (s32[]{:T(128)}, f32[1024,2048]{1,0:T(8,128)}, f32[2,1024,64]{2,1,0:T(8,128)S(1)}, f32[2,64,64]{2,1,0:T(8,128)S(1)}, s32[]{:T(128)}, /*index=5*/s32[]{:T(128)}, s32[]{:T(128)}) while((s32[]{:T(128)}, f32[1024,2048]{1,0:T(8,128)}, f32[2,1024,64]{2,1,0:T(8,128)S(1)}, f32[2,64,64]{2,1,0:T(8,128)S(1)}, s32[]{:T(128)}, ...), condition=%wide.region_3.3_spmd, body=%wide.region_1.2_spmd.sunk | while | flops 3324116992 | bytes 31490224 | solution.py:34
  2683.4 33.9 all-reduce.2.cloned.1.call-done
  2738.1 33.9 all-reduce.2.cloned.1.call-done
  2790.8 109.2 %while.45 = (s32[]{:T(128)}, f32[1024,2048]{1,0:T(8,128)}, f32[2,1024,64]{2,1,0:T(8,128)S(1)}, f32[2,64,64]{2,1,0:T(8,128)S(1)}, s32[]{:T(128)}, /*index=5*/s32[]{:T(128)}, s32[]{:T(128)}) while((s32[]{:T(128)}, f32[1024,2048]{1,0:T(8,128)}, f32[2,1024,64]{2,1,0:T(8,128)S(1)}, f32[2,64,64]{2,1,0:T(8,128)S(1)}, s32[]{:T(128)}, ...), condition=%wide.region_3.3_spmd, body=%wide.region_1.2_spmd.sunk | while | flops 3324116992 | bytes 31490224 | solution.py:34
  2906.4 109.3 %while.45 = (s32[]{:T(128)}, f32[1024,2048]{1,0:T(8,128)}, f32[2,1024,64]{2,1,0:T(8,128)S(1)}, f32[2,64,64]{2,1,0:T(8,128)S(1)}, s32[]{:T(128)}, /*index=5*/s32[]{:T(128)}, s32[]{:T(128)}) while((s32[]{:T(128)}, f32[1024,2048]{1,0:T(8,128)}, f32[2,1024,64]{2,1,0:T(8,128)S(1)}, f32[2,64,64]{2,1,0:T(8,128)S(1)}, s32[]{:T(128)}, ...), condition=%wide.region_3.3_spmd, body=%wide.region_1.2_spmd.sunk | while | flops 3324116992 | bytes 31490224 | solution.py:34
  2914.8 33.9 all-reduce.2.cloned.1.call-done
  3022.1 109.2 %while.45 = (s32[]{:T(128)}, f32[1024,2048]{1,0:T(8,128)}, f32[2,1024,64]{2,1,0:T(8,128)S(1)}, f32[2,64,64]{2,1,0:T(8,128)S(1)}, s32[]{:T(128)}, /*index=5*/s32[]{:T(128)}, s32[]{:T(128)}) while((s32[]{:T(128)}, f32[1024,2048]{1,0:T(8,128)}, f32[2,1024,64]{2,1,0:T(8,128)S(1)}, f32[2,64,64]{2,1,0:T(8,128)S(1)}, s32[]{:T(128)}, ...), condition=%wide.region_3.3_spmd, body=%wide.region_1.2_spmd.sunk | while | flops 3324116992 | bytes 31490224 | solution.py:34
  3137.8 109.3 %while.45 = (s32[]{:T(128)}, f32[1024,2048]{1,0:T(8,128)}, f32[2,1024,64]{2,1,0:T(8,128)S(1)}, f32[2,64,64]{2,1,0:T(8,128)S(1)}, s32[]{:T(128)}, /*index=5*/s32[]{:T(128)}, s32[]{:T(128)}) while((s32[]{:T(128)}, f32[1024,2048]{1,0:T(8,128)}, f32[2,1024,64]{2,1,0:T(8,128)S(1)}, f32[2,64,64]{2,1,0:T(8,128)S(1)}, s32[]{:T(128)}, ...), condition=%wide.region_3.3_spmd, body=%wide.region_1.2_spmd.sunk | while | flops 3324116992 | bytes 31490224 | solution.py:34
  3146.1 33.9 all-reduce.2.cloned.1.call-done
  3200.7 33.9 all-reduce.2.cloned.1.call-done
  3253.4 109.2 %while.45 = (s32[]{:T(128)}, f32[1024,2048]{1,0:T(8,128)}, f32[2,1024,64]{2,1,0:T(8,128)S(1)}, f32[2,64,64]{2,1,0:T(8,128)S(1)}, s32[]{:T(128)}, /*index=5*/s32[]{:T(128)}, s32[]{:T(128)}) while((s32[]{:T(128)}, f32[1024,2048]{1,0:T(8,128)}, f32[2,1024,64]{2,1,0:T(8,128)S(1)}, f32[2,64,64]{2,1,0:T(8,128)S(1)}, s32[]{:T(128)}, ...), condition=%wide.region_3.3_spmd, body=%wide.region_1.2_spmd.sunk | while | flops 3324116992 | bytes 31490224 | solution.py:34
  3369.1 109.3 %while.45 = (s32[]{:T(128)}, f32[1024,2048]{1,0:T(8,128)}, f32[2,1024,64]{2,1,0:T(8,128)S(1)}, f32[2,64,64]{2,1,0:T(8,128)S(1)}, s32[]{:T(128)}, /*index=5*/s32[]{:T(128)}, s32[]{:T(128)}) while((s32[]{:T(128)}, f32[1024,2048]{1,0:T(8,128)}, f32[2,1024,64]{2,1,0:T(8,128)S(1)}, f32[2,64,64]{2,1,0:T(8,128)S(1)}, s32[]{:T(128)}, ...), condition=%wide.region_3.3_spmd, body=%wide.region_1.2_spmd.sunk | while | flops 3324116992 | bytes 31490224 | solution.py:34
  3377.4 33.9 all-reduce.2.cloned.1.call-done
  3484.7 109.2 %while.45 = (s32[]{:T(128)}, f32[1024,2048]{1,0:T(8,128)}, f32[2,1024,64]{2,1,0:T(8,128)S(1)}, f32[2,64,64]{2,1,0:T(8,128)S(1)}, s32[]{:T(128)}, /*index=5*/s32[]{:T(128)}, s32[]{:T(128)}) while((s32[]{:T(128)}, f32[1024,2048]{1,0:T(8,128)}, f32[2,1024,64]{2,1,0:T(8,128)S(1)}, f32[2,64,64]{2,1,0:T(8,128)S(1)}, s32[]{:T(128)}, ...), condition=%wide.region_3.3_spmd, body=%wide.region_1.2_spmd.sunk | while | flops 3324116992 | bytes 31490224 | solution.py:34
  3600.4 109.3 %while.45 = (s32[]{:T(128)}, f32[1024,2048]{1,0:T(8,128)}, f32[2,1024,64]{2,1,0:T(8,128)S(1)}, f32[2,64,64]{2,1,0:T(8,128)S(1)}, s32[]{:T(128)}, /*index=5*/s32[]{:T(128)}, s32[]{:T(128)}) while((s32[]{:T(128)}, f32[1024,2048]{1,0:T(8,128)}, f32[2,1024,64]{2,1,0:T(8,128)S(1)}, f32[2,64,64]{2,1,0:T(8,128)S(1)}, s32[]{:T(128)}, ...), condition=%wide.region_3.3_spmd, body=%wide.region_1.2_spmd.sunk | while | flops 3324116992 | bytes 31490224 | solution.py:34
  3608.7 33.9 all-reduce.2.cloned.1.call-done
  3716.1 109.2 %while.45 = (s32[]{:T(128)}, f32[1024,2048]{1,0:T(8,128)}, f32[2,1024,64]{2,1,0:T(8,128)S(1)}, f32[2,64,64]{2,1,0:T(8,128)S(1)}, s32[]{:T(128)}, /*index=5*/s32[]{:T(128)}, s32[]{:T(128)}) while((s32[]{:T(128)}, f32[1024,2048]{1,0:T(8,128)}, f32[2,1024,64]{2,1,0:T(8,128)S(1)}, f32[2,64,64]{2,1,0:T(8,128)S(1)}, s32[]{:T(128)}, ...), condition=%wide.region_3.3_spmd, body=%wide.region_1.2_spmd.sunk | while | flops 3324116992 | bytes 31490224 | solution.py:34
  3829.7 95.5 %all_to_all.38 = f32[1024,4,512]{2,0,1:T(8,128)S(1)} all-to-all(f32[1024,4,512]{2,0,1:T(8,128)S(1)} %bitcast.40), channel_id=1, replica_groups=mesh['row'=4,'col'=2] {'row'}, dimensions={1} | all-to-all | bytes 16777216 | tf_op jit(solution)/shard_map/all_to_all | solution.py:37
  (488 shorter events, 2749.2 us)
Async XLA Ops:
  6.5 99.6 %all-to-all-start = ((f32[4,1024,512]{2,1,0:T(8,128)}), f32[4,1024,512]{2,1,0:T(8,128)}, u32[]{:S(2)}, u32[]{:S(2)}) async-start(f32[4,1024,512]{2,1,0:T(8,128)} %bitcast.42), calls=%async_computation | async-start | bytes 16777216 | tf_op jit(solution)/shard_map/all_to_all | solution.py:16
  130.5 42.3 %all-reduce.2.cloned.1.call-start = ((), (), s32[]{:S(2)}) async-start(), calls=%async_computation.2 | async-start | bytes 1048576 | tf_op jit(solution)/shard_map/while/body/eval_jaxpr/while/body/eval_jaxpr/psum | solution.py:30
  185.3 42.2 %all-reduce.2.cloned.1.call-start = ((), (), s32[]{:S(2)}) async-start(), calls=%async_computation.2 | async-start | bytes 1048576 | tf_op jit(solution)/shard_map/while/body/eval_jaxpr/while/body/eval_jaxpr/psum | solution.py:30
  246.3 42.2 %all-reduce.2.cloned.1.call-start = ((), (), s32[]{:S(2)}) async-start(), calls=%async_computation.2 | async-start | bytes 1048576 | tf_op jit(solution)/shard_map/while/body/eval_jaxpr/while/body/eval_jaxpr/psum | solution.py:30
  300.9 42.2 %all-reduce.2.cloned.1.call-start = ((), (), s32[]{:S(2)}) async-start(), calls=%async_computation.2 | async-start | bytes 1048576 | tf_op jit(solution)/shard_map/while/body/eval_jaxpr/while/body/eval_jaxpr/psum | solution.py:30
  362.0 42.2 %all-reduce.2.cloned.1.call-start = ((), (), s32[]{:S(2)}) async-start(), calls=%async_computation.2 | async-start | bytes 1048576 | tf_op jit(solution)/shard_map/while/body/eval_jaxpr/while/body/eval_jaxpr/psum | solution.py:30
  416.6 42.2 %all-reduce.2.cloned.1.call-start = ((), (), s32[]{:S(2)}) async-start(), calls=%async_computation.2 | async-start | bytes 1048576 | tf_op jit(solution)/shard_map/while/body/eval_jaxpr/while/body/eval_jaxpr/psum | solution.py:30
  477.6 42.2 %all-reduce.2.cloned.1.call-start = ((), (), s32[]{:S(2)}) async-start(), calls=%async_computation.2 | async-start | bytes 1048576 | tf_op jit(solution)/shard_map/while/body/eval_jaxpr/while/body/eval_jaxpr/psum | solution.py:30
  532.2 42.2 %all-reduce.2.cloned.1.call-start = ((), (), s32[]{:S(2)}) async-start(), calls=%async_computation.2 | async-start | bytes 1048576 | tf_op jit(solution)/shard_map/while/body/eval_jaxpr/while/body/eval_jaxpr/psum | solution.py:30
  593.3 42.2 %all-reduce.2.cloned.1.call-start = ((), (), s32[]{:S(2)}) async-start(), calls=%async_computation.2 | async-start | bytes 1048576 | tf_op jit(solution)/shard_map/while/body/eval_jaxpr/while/body/eval_jaxpr/psum | solution.py:30
  647.9 42.2 %all-reduce.2.cloned.1.call-start = ((), (), s32[]{:S(2)}) async-start(), calls=%async_computation.2 | async-start | bytes 1048576 | tf_op jit(solution)/shard_map/while/body/eval_jaxpr/while/body/eval_jaxpr/psum | solution.py:30
  708.9 42.2 %all-reduce.2.cloned.1.call-start = ((), (), s32[]{:S(2)}) async-start(), calls=%async_computation.2 | async-start | bytes 1048576 | tf_op jit(solution)/shard_map/while/body/eval_jaxpr/while/body/eval_jaxpr/psum | solution.py:30
  763.6 42.2 %all-reduce.2.cloned.1.call-start = ((), (), s32[]{:S(2)}) async-start(), calls=%async_computation.2 | async-start | bytes 1048576 | tf_op jit(solution)/shard_map/while/body/eval_jaxpr/while/body/eval_jaxpr/psum | solution.py:30
  824.6 42.2 %all-reduce.2.cloned.1.call-start = ((), (), s32[]{:S(2)}) async-start(), calls=%async_computation.2 | async-start | bytes 1048576 | tf_op jit(solution)/shard_map/while/body/eval_jaxpr/while/body/eval_jaxpr/psum | solution.py:30
  879.2 42.2 %all-reduce.2.cloned.1.call-start = ((), (), s32[]{:S(2)}) async-start(), calls=%async_computation.2 | async-start | bytes 1048576 | tf_op jit(solution)/shard_map/while/body/eval_jaxpr/while/body/eval_jaxpr/psum | solution.py:30
  940.2 42.2 %all-reduce.2.cloned.1.call-start = ((), (), s32[]{:S(2)}) async-start(), calls=%async_computation.2 | async-start | bytes 1048576 | tf_op jit(solution)/shard_map/while/body/eval_jaxpr/while/body/eval_jaxpr/psum | solution.py:30
  994.9 42.2 %all-reduce.2.cloned.1.call-start = ((), (), s32[]{:S(2)}) async-start(), calls=%async_computation.2 | async-start | bytes 1048576 | tf_op jit(solution)/shard_map/while/body/eval_jaxpr/while/body/eval_jaxpr/psum | solution.py:30
  1055.9 42.2 %all-reduce.2.cloned.1.call-start = ((), (), s32[]{:S(2)}) async-start(), calls=%async_computation.2 | async-start | bytes 1048576 | tf_op jit(solution)/shard_map/while/body/eval_jaxpr/while/body/eval_jaxpr/psum | solution.py:30
  1110.5 42.2 %all-reduce.2.cloned.1.call-start = ((), (), s32[]{:S(2)}) async-start(), calls=%async_computation.2 | async-start | bytes 1048576 | tf_op jit(solution)/shard_map/while/body/eval_jaxpr/while/body/eval_jaxpr/psum | solution.py:30
  1171.6 42.2 %all-reduce.2.cloned.1.call-start = ((), (), s32[]{:S(2)}) async-start(), calls=%async_computation.2 | async-start | bytes 1048576 | tf_op jit(solution)/shard_map/while/body/eval_jaxpr/while/body/eval_jaxpr/psum | solution.py:30
  1226.2 42.2 %all-reduce.2.cloned.1.call-start = ((), (), s32[]{:S(2)}) async-start(), calls=%async_computation.2 | async-start | bytes 1048576 | tf_op jit(solution)/shard_map/while/body/eval_jaxpr/while/body/eval_jaxpr/psum | solution.py:30
  1287.2 42.2 %all-reduce.2.cloned.1.call-start = ((), (), s32[]{:S(2)}) async-start(), calls=%async_computation.2 | async-start | bytes 1048576 | tf_op jit(solution)/shard_map/while/body/eval_jaxpr/while/body/eval_jaxpr/psum | solution.py:30
  1341.9 42.2 %all-reduce.2.cloned.1.call-start = ((), (), s32[]{:S(2)}) async-start(), calls=%async_computation.2 | async-start | bytes 1048576 | tf_op jit(solution)/shard_map/while/body/eval_jaxpr/while/body/eval_jaxpr/psum | solution.py:30
  1402.9 42.2 %all-reduce.2.cloned.1.call-start = ((), (), s32[]{:S(2)}) async-start(), calls=%async_computation.2 | async-start | bytes 1048576 | tf_op jit(solution)/shard_map/while/body/eval_jaxpr/while/body/eval_jaxpr/psum | solution.py:30
  1457.5 42.2 %all-reduce.2.cloned.1.call-start = ((), (), s32[]{:S(2)}) async-start(), calls=%async_computation.2 | async-start | bytes 1048576 | tf_op jit(solution)/shard_map/while/body/eval_jaxpr/while/body/eval_jaxpr/psum | solution.py:30
  1518.5 42.2 %all-reduce.2.cloned.1.call-start = ((), (), s32[]{:S(2)}) async-start(), calls=%async_computation.2 | async-start | bytes 1048576 | tf_op jit(solution)/shard_map/while/body/eval_jaxpr/while/body/eval_jaxpr/psum | solution.py:30
  1573.2 42.2 %all-reduce.2.cloned.1.call-start = ((), (), s32[]{:S(2)}) async-start(), calls=%async_computation.2 | async-start | bytes 1048576 | tf_op jit(solution)/shard_map/while/body/eval_jaxpr/while/body/eval_jaxpr/psum | solution.py:30
  1634.2 42.2 %all-reduce.2.cloned.1.call-start = ((), (), s32[]{:S(2)}) async-start(), calls=%async_computation.2 | async-start | bytes 1048576 | tf_op jit(solution)/shard_map/while/body/eval_jaxpr/while/body/eval_jaxpr/psum | solution.py:30
  1688.8 42.2 %all-reduce.2.cloned.1.call-start = ((), (), s32[]{:S(2)}) async-start(), calls=%async_computation.2 | async-start | bytes 1048576 | tf_op jit(solution)/shard_map/while/body/eval_jaxpr/while/body/eval_jaxpr/psum | solution.py:30
  1749.9 42.2 %all-reduce.2.cloned.1.call-start = ((), (), s32[]{:S(2)}) async-start(), calls=%async_computation.2 | async-start | bytes 1048576 | tf_op jit(solution)/shard_map/while/body/eval_jaxpr/while/body/eval_jaxpr/psum | solution.py:30
  1804.5 42.2 %all-reduce.2.cloned.1.call-start = ((), (), s32[]{:S(2)}) async-start(), calls=%async_computation.2 | async-start | bytes 1048576 | tf_op jit(solution)/shard_map/while/body/eval_jaxpr/while/body/eval_jaxpr/psum | solution.py:30
  1865.5 42.2 %all-reduce.2.cloned.1.call-start = ((), (), s32[]{:S(2)}) async-start(), calls=%async_computation.2 | async-start | bytes 1048576 | tf_op jit(solution)/shard_map/while/body/eval_jaxpr/while/body/eval_jaxpr/psum | solution.py:30
  1920.1 42.2 %all-reduce.2.cloned.1.call-start = ((), (), s32[]{:S(2)}) async-start(), calls=%async_computation.2 | async-start | bytes 1048576 | tf_op jit(solution)/shard_map/while/body/eval_jaxpr/while/body/eval_jaxpr/psum | solution.py:30
  1981.2 42.2 %all-reduce.2.cloned.1.call-start = ((), (), s32[]{:S(2)}) async-start(), calls=%async_computation.2 | async-start | bytes 1048576 | tf_op jit(solution)/shard_map/while/body/eval_jaxpr/while/body/eval_jaxpr/psum | solution.py:30
  2035.8 42.2 %all-reduce.2.cloned.1.call-start = ((), (), s32[]{:S(2)}) async-start(), calls=%async_computation.2 | async-start | bytes 1048576 | tf_op jit(solution)/shard_map/while/body/eval_jaxpr/while/body/eval_jaxpr/psum | solution.py:30
  2096.8 42.2 %all-reduce.2.cloned.1.call-start = ((), (), s32[]{:S(2)}) async-start(), calls=%async_computation.2 | async-start | bytes 1048576 | tf_op jit(solution)/shard_map/while/body/eval_jaxpr/while/body/eval_jaxpr/psum | solution.py:30
  2151.5 42.2 %all-reduce.2.cloned.1.call-start = ((), (), s32[]{:S(2)}) async-start(), calls=%async_computation.2 | async-start | bytes 1048576 | tf_op jit(solution)/shard_map/while/body/eval_jaxpr/while/body/eval_jaxpr/psum | solution.py:30
  2212.5 42.2 %all-reduce.2.cloned.1.call-start = ((), (), s32[]{:S(2)}) async-start(), calls=%async_computation.2 | async-start | bytes 1048576 | tf_op jit(solution)/shard_map/while/body/eval_jaxpr/while/body/eval_jaxpr/psum | solution.py:30
  2267.1 42.2 %all-reduce.2.cloned.1.call-start = ((), (), s32[]{:S(2)}) async-start(), calls=%async_computation.2 | async-start | bytes 1048576 | tf_op jit(solution)/shard_map/while/body/eval_jaxpr/while/body/eval_jaxpr/psum | solution.py:30
  2328.2 42.2 %all-reduce.2.cloned.1.call-start = ((), (), s32[]{:S(2)}) async-start(), calls=%async_computation.2 | async-start | bytes 1048576 | tf_op jit(solution)/shard_map/while/body/eval_jaxpr/while/body/eval_jaxpr/psum | solution.py:30
  2382.8 42.2 %all-reduce.2.cloned.1.call-start = ((), (), s32[]{:S(2)}) async-start(), calls=%async_computation.2 | async-start | bytes 1048576 | tf_op jit(solution)/shard_map/while/body/eval_jaxpr/while/body/eval_jaxpr/psum | solution.py:30
  2443.8 42.2 %all-reduce.2.cloned.1.call-start = ((), (), s32[]{:S(2)}) async-start(), calls=%async_computation.2 | async-start | bytes 1048576 | tf_op jit(solution)/shard_map/while/body/eval_jaxpr/while/body/eval_jaxpr/psum | solution.py:30
  2498.4 42.2 %all-reduce.2.cloned.1.call-start = ((), (), s32[]{:S(2)}) async-start(), calls=%async_computation.2 | async-start | bytes 1048576 | tf_op jit(solution)/shard_map/while/body/eval_jaxpr/while/body/eval_jaxpr/psum | solution.py:30
  2559.5 42.2 %all-reduce.2.cloned.1.call-start = ((), (), s32[]{:S(2)}) async-start(), calls=%async_computation.2 | async-start | bytes 1048576 | tf_op jit(solution)/shard_map/while/body/eval_jaxpr/while/body/eval_jaxpr/psum | solution.py:30
  2614.1 42.2 %all-reduce.2.cloned.1.call-start = ((), (), s32[]{:S(2)}) async-start(), calls=%async_computation.2 | async-start | bytes 1048576 | tf_op jit(solution)/shard_map/while/body/eval_jaxpr/while/body/eval_jaxpr/psum | solution.py:30
  2675.1 42.2 %all-reduce.2.cloned.1.call-start = ((), (), s32[]{:S(2)}) async-start(), calls=%async_computation.2 | async-start | bytes 1048576 | tf_op jit(solution)/shard_map/while/body/eval_jaxpr/while/body/eval_jaxpr/psum | solution.py:30
  2729.8 42.2 %all-reduce.2.cloned.1.call-start = ((), (), s32[]{:S(2)}) async-start(), calls=%async_computation.2 | async-start | bytes 1048576 | tf_op jit(solution)/shard_map/while/body/eval_jaxpr/while/body/eval_jaxpr/psum | solution.py:30
  2790.8 42.2 %all-reduce.2.cloned.1.call-start = ((), (), s32[]{:S(2)}) async-start(), calls=%async_computation.2 | async-start | bytes 1048576 | tf_op jit(solution)/shard_map/while/body/eval_jaxpr/while/body/eval_jaxpr/psum | solution.py:30
  2845.4 42.2 %all-reduce.2.cloned.1.call-start = ((), (), s32[]{:S(2)}) async-start(), calls=%async_computation.2 | async-start | bytes 1048576 | tf_op jit(solution)/shard_map/while/body/eval_jaxpr/while/body/eval_jaxpr/psum | solution.py:30
  2906.4 42.2 %all-reduce.2.cloned.1.call-start = ((), (), s32[]{:S(2)}) async-start(), calls=%async_computation.2 | async-start | bytes 1048576 | tf_op jit(solution)/shard_map/while/body/eval_jaxpr/while/body/eval_jaxpr/psum | solution.py:30
  2961.1 42.2 %all-reduce.2.cloned.1.call-start = ((), (), s32[]{:S(2)}) async-start(), calls=%async_computation.2 | async-start | bytes 1048576 | tf_op jit(solution)/shard_map/while/body/eval_jaxpr/while/body/eval_jaxpr/psum | solution.py:30
  3022.1 42.2 %all-reduce.2.cloned.1.call-start = ((), (), s32[]{:S(2)}) async-start(), calls=%async_computation.2 | async-start | bytes 1048576 | tf_op jit(solution)/shard_map/while/body/eval_jaxpr/while/body/eval_jaxpr/psum | solution.py:30
  3076.7 42.2 %all-reduce.2.cloned.1.call-start = ((), (), s32[]{:S(2)}) async-start(), calls=%async_computation.2 | async-start | bytes 1048576 | tf_op jit(solution)/shard_map/while/body/eval_jaxpr/while/body/eval_jaxpr/psum | solution.py:30
  3137.8 42.2 %all-reduce.2.cloned.1.call-start = ((), (), s32[]{:S(2)}) async-start(), calls=%async_computation.2 | async-start | bytes 1048576 | tf_op jit(solution)/shard_map/while/body/eval_jaxpr/while/body/eval_jaxpr/psum | solution.py:30
  3192.4 42.2 %all-reduce.2.cloned.1.call-start = ((), (), s32[]{:S(2)}) async-start(), calls=%async_computation.2 | async-start | bytes 1048576 | tf_op jit(solution)/shard_map/while/body/eval_jaxpr/while/body/eval_jaxpr/psum | solution.py:30
  3253.4 42.2 %all-reduce.2.cloned.1.call-start = ((), (), s32[]{:S(2)}) async-start(), calls=%async_computation.2 | async-start | bytes 1048576 | tf_op jit(solution)/shard_map/while/body/eval_jaxpr/while/body/eval_jaxpr/psum | solution.py:30
  3308.1 42.2 %all-reduce.2.cloned.1.call-start = ((), (), s32[]{:S(2)}) async-start(), calls=%async_computation.2 | async-start | bytes 1048576 | tf_op jit(solution)/shard_map/while/body/eval_jaxpr/while/body/eval_jaxpr/psum | solution.py:30
  3369.1 42.2 %all-reduce.2.cloned.1.call-start = ((), (), s32[]{:S(2)}) async-start(), calls=%async_computation.2 | async-start | bytes 1048576 | tf_op jit(solution)/shard_map/while/body/eval_jaxpr/while/body/eval_jaxpr/psum | solution.py:30
  3423.7 42.2 %all-reduce.2.cloned.1.call-start = ((), (), s32[]{:S(2)}) async-start(), calls=%async_computation.2 | async-start | bytes 1048576 | tf_op jit(solution)/shard_map/while/body/eval_jaxpr/while/body/eval_jaxpr/psum | solution.py:30
  3484.7 42.2 %all-reduce.2.cloned.1.call-start = ((), (), s32[]{:S(2)}) async-start(), calls=%async_computation.2 | async-start | bytes 1048576 | tf_op jit(solution)/shard_map/while/body/eval_jaxpr/while/body/eval_jaxpr/psum | solution.py:30
  3539.4 42.2 %all-reduce.2.cloned.1.call-start = ((), (), s32[]{:S(2)}) async-start(), calls=%async_computation.2 | async-start | bytes 1048576 | tf_op jit(solution)/shard_map/while/body/eval_jaxpr/while/body/eval_jaxpr/psum | solution.py:30
  3600.4 42.2 %all-reduce.2.cloned.1.call-start = ((), (), s32[]{:S(2)}) async-start(), calls=%async_computation.2 | async-start | bytes 1048576 | tf_op jit(solution)/shard_map/while/body/eval_jaxpr/while/body/eval_jaxpr/psum | solution.py:30
  3655.0 42.2 %all-reduce.2.cloned.1.call-start = ((), (), s32[]{:S(2)}) async-start(), calls=%async_computation.2 | async-start | bytes 1048576 | tf_op jit(solution)/shard_map/while/body/eval_jaxpr/while/body/eval_jaxpr/psum | solution.py:30
  3716.1 42.2 %all-reduce.2.cloned.1.call-start = ((), (), s32[]{:S(2)}) async-start(), calls=%async_computation.2 | async-start | bytes 1048576 | tf_op jit(solution)/shard_map/while/body/eval_jaxpr/while/body/eval_jaxpr/psum | solution.py:30
  (1 other events, 42.2 us)
Sparse Core Ops, SparseCore 0:
  138.9 33.8 all-reduce.1
  193.7 33.6 all-reduce.1
  254.7 33.6 all-reduce.1
  309.4 33.6 all-reduce.1
  370.4 33.6 all-reduce.1
  425.0 33.6 all-reduce.1
  486.0 33.6 all-reduce.1
  540.7 33.6 all-reduce.1
  601.7 33.6 all-reduce.1
  656.3 33.6 all-reduce.1
  717.4 33.6 all-reduce.1
  772.0 33.6 all-reduce.1
  833.0 33.6 all-reduce.1
  887.6 33.6 all-reduce.1
  948.7 33.6 all-reduce.1
  1003.3 33.6 all-reduce.1
  1064.3 33.6 all-reduce.1
  1119.0 33.6 all-reduce.1
  1180.0 33.6 all-reduce.1
  1234.6 33.6 all-reduce.1
  1295.7 33.6 all-reduce.1
  1350.3 33.6 all-reduce.1
  1411.3 33.6 all-reduce.1
  1465.9 33.6 all-reduce.1
  1527.0 33.6 all-reduce.1
  1581.6 33.6 all-reduce.1
  1642.6 33.6 all-reduce.1
  1697.3 33.6 all-reduce.1
  1758.3 33.6 all-reduce.1
  1812.9 33.6 all-reduce.1
  1874.0 33.6 all-reduce.1
  1928.6 33.6 all-reduce.1
  1989.6 33.6 all-reduce.1
  2044.2 33.6 all-reduce.1
  2105.3 33.6 all-reduce.1
  2159.9 33.6 all-reduce.1
  2220.9 33.6 all-reduce.1
  2275.6 33.6 all-reduce.1
  2336.6 33.6 all-reduce.1
  2391.2 33.6 all-reduce.1
  2452.2 33.6 all-reduce.1
  2506.9 33.6 all-reduce.1
  2567.9 33.6 all-reduce.1
  2622.5 33.6 all-reduce.1
  2683.6 33.6 all-reduce.1
  2738.2 33.6 all-reduce.1
  2799.2 33.6 all-reduce.1
  2853.9 33.6 all-reduce.1
  2914.9 33.6 all-reduce.1
  2969.5 33.6 all-reduce.1
  3030.5 33.6 all-reduce.1
  3085.2 33.6 all-reduce.1
  3146.2 33.6 all-reduce.1
  3200.8 33.6 all-reduce.1
  3261.9 33.6 all-reduce.1
  3316.5 33.6 all-reduce.1
  3377.5 33.6 all-reduce.1
  3432.1 33.6 all-reduce.1
  3493.2 33.6 all-reduce.1
  3547.8 33.6 all-reduce.1
  3608.8 33.6 all-reduce.1
  3663.5 33.6 all-reduce.1
  3724.5 33.6 all-reduce.1
  3779.1 33.6 all-reduce.1
where the time goes:
time: 3950 us; the launch traced here: 3940 us
  waiting for transfers between devices  2260 us (57%)
  matrix products  1330 us (34%)
  blocking collectives  236 us (6%)
  local copies, waits for them, and re-layouts  89.6 us (2%)
    psum x64, waiting for transfers between devices, inner_step(): w_sum = lax.psum(w_part, 'row')  2170 us
    dot_general x64, matrix products, inner_step(): jnp.dot(v_blk, y_blk, precision=FULL_PREC, preferred_element_type=jnp.flo...  695 us
    dot_general x64, matrix products, inner_step(): lax.dot_general(v_blk, x_in, CONTRACT_ROWS, precision=FULL_PREC, preferre...  530 us
    dot_general x64, matrix products, inner_step(): jnp.dot(t_blk, w_sum, precision=FULL_PREC, preferred_element_type=jnp.flo...  102 us
    all_to_all x1, blocking collectives, local_apply(): return lax.all_to_all(x_two, 'row', 1, 0, tiled=True)  95.5 us
    all_to_all x1, waiting for transfers between devices, local_apply(): x_two = lax.all_to_all(z_loc, 'row', 0, 1, tiled=True)  94 us
    all_gather x32, blocking collectives, outer_step(): v_all = lax.all_gather(v_own, 'col')  81.9 us
  transfers between devices with their start and end apart: 65, of which 65 were waited for; matrix products, arithmetic and copies ran while one was open for 0% of the time, Pallas kernels for 0%

commit v1 on v0

v1 whole, which is shorter than its diff:
```python
import functools

import jax
import jax.numpy as jnp
from jax import lax
from jax.experimental import pallas as pl
from jax.experimental.pallas import tpu as pltpu
from jax.sharding import PartitionSpec as P

MESH = pl.DeviceIdType.MESH
F32 = jnp.float32
BF16 = jnp.bfloat16

NU = 16
NCH = NU * (NU + 1) // 2
L0, L1, L2 = 12, 7, 3
EXTRA = 24


def split3(x):
    h = x.astype(BF16)
    rem = x - h.astype(F32)
    m = rem.astype(BF16)
    l = (rem - m.astype(F32)).astype(BF16)
    return h, m, l


def dot(a, b):
    return jnp.dot(a, b, preferred_element_type=F32)


def mm6(a, b):
    ah, am, al = a
    bh, bm, bl = b
    return (dot(al, bh) + dot(ah, bl) + dot(am, bm)) + (dot(am, bh) + dot(ah, bm)) + dot(ah, bh)


def mm_f32(a, b):
    return mm6(split3(a), split3(b))


def kernel(
    v_hbm, d_hbm, z_hbm, out_hbm,
    vbuf, xbuf, dbuf, vt3, vn3, x3, y3, wacc, s1acc, s2acc, tmat,
    r1_sem, r2_sem, rd_sem, rp_sem, loc_sem, send_sem, z_sem, d_sem, o_sem,
):
    r = lax.axis_index("row")
    q = lax.axis_index("col")
    ry, rx = r // 2, r % 2
    row_x = ry * 2 + (1 - rx)
    row_y = (1 - ry) * 2 + rx
    n1 = row_x * (1 - q) + row_y * q
    n2 = row_y * (1 - q) + row_x * q
    nd = 3 - r
    dev1, dev2, devp = (n1, q), (n2, q), (r, 1 - q)
    cols = pl.ds(pl.multiple_of(q * 128, 128), 128)

    def piece(c, rr):
        return vbuf.at[c, pl.ds(pl.multiple_of(rr * 64, 64), 64), cols]

    def remote(src, dst, k, rsem, dev):
        return pltpu.make_async_remote_copy(
            src_ref=src, dst_ref=dst, send_sem=send_sem.at[k], recv_sem=rsem,
            device_id=dev, device_id_type=MESH,
        )

    def own_src(s, u):
        return v_hbm.at[u, :, pl.ds(pl.multiple_of(s * 128, 128), 128)]

    def stage0(c, s, u):
        src = own_src(s, u)
        remote(src, piece(c, r), 0, r1_sem.at[c], dev1).start()
        remote(src, piece(c, r), 1, r2_sem.at[c], dev2).start()
        pltpu.make_async_copy(src, piece(c, r), loc_sem.at[c]).start()

    def stage1(c):
        p = piece(c, n1)
        remote(p, p, 0, r1_sem.at[c], dev1).wait_recv()
        remote(p, p, 2, rd_sem.at[c], dev2).start()

    def stage2(c):
        p = piece(c, n2)
        remote(p, p, 1, r2_sem.at[c], dev2).wait_recv()
        p = piece(c, nd)
        remote(p, p, 2, rd_sem.at[c], dev2).wait_recv()
        p = piece(c, r)
        pltpu.make_async_copy(p, p, loc_sem.at[c]).wait()
        p = vbuf.at[c, :, cols]
        remote(p, p, 3, rp_sem.at[c], devp).start()

    def stage3(c):
        p = vbuf.at[c, :, pl.ds(pl.multiple_of((1 - q) * 128, 128), 128)]
        remote(p, p, 3, rp_sem.at[c], devp).wait_recv()

    def comm_tick(n, su):
        s, u = su

        @pl.when(n + L0 < NCH)
        def _():
            stage0(n + L0, s, u)

        @pl.when(jnp.logical_and(n + L1 >= 0, n + L1 < NCH))
        def _():
            stage1(n + L1)

        @pl.when(jnp.logical_and(n + L2 >= 0, n + L2 < NCH))
        def _():
            stage2(n + L2)

        last = u == NU - 1
        s2 = jnp.where(last, jnp.maximum(s - 1, 0), s)
        u2 = jnp.where(last, s2, u + 1)
        return s2, u2

    def tick(c, carry):
        n, s, u = carry
        count = jnp.where(c < EXTRA, 2, 1)
        s, u = lax.fori_loop(0, count, lambda i, su: comm_tick(n + i, su), (s, u))
        stage3(c)
        return n + count, s, u

    barrier = pltpu.get_barrier_semaphore()
    for dev in (dev1, dev2, devp):
        pl.semaphore_signal(barrier, inc=1, device_id=dev, device_id_type=MESH)
    pl.semaphore_wait(barrier, 3)

    d_own = dbuf.at[q]
    d_send = pltpu.make_async_remote_copy(
        src_ref=d_hbm, dst_ref=d_own, send_sem=d_sem.at[0], recv_sem=d_sem.at[1],
        device_id=devp, device_id_type=MESH,
    )
    d_send.start()
    d_loc = pltpu.make_async_copy(d_hbm, d_own, d_sem.at[2])
    d_loc.start()

    def z_copy(u):
        return pltpu.make_async_copy(z_hbm.at[:, u], xbuf.at[u], z_sem.at[u])

    s0, u0 = lax.fori_loop(-L0, 0, comm_tick, (jnp.int32(NU - 1), jnp.int32(NU - 1)))
    lax.fori_loop(0, NU, lambda i, _: (z_copy(NU - 1 - i).start(), 0)[1], 0)
    d_send.wait()
    d_loc.wait()

    def do_a(c, u):
        v = vbuf[c]
        th, tm, tl = split3(v.T)
        vt3[0], vt3[1], vt3[2] = th, tm, tl
        nh, nm, nl = split3(v)
        vn3[0], vn3[1], vn3[2] = nh, nm, nl
        xh, xm, xl = split3(xbuf[u].reshape(256, 512))
        x3[0], x3[1], x3[2] = xh, xm, xl
        wacc[...] += mm6((vt3[0], vt3[1], vt3[2]), (x3[0], x3[1], x3[2]))
        s1acc[...] += dot(vt3[1], vn3[1]) + dot(vt3[0], vn3[0])
        s2acc[...] += dot(vt3[0], vn3[2]) + dot(vt3[0], vn3[1])

    def do_c(c, u):
        upd = mm6(split3(vbuf[c]), (y3[0], y3[1], y3[2]))
        xbuf[u] = xbuf[u] - upd.reshape(4, 64, 512)

    lane = lax.broadcasted_iota(jnp.int32, (64, 128), 1)
    low = lane < 64

    def roll(x):
        return pltpu.roll(x, 64, 1)

    def merge_t(s):
        s2 = s2acc[...]
        g = s1acc[...] + s2 + s2.T
        da, db = dbuf[0, s], dbuf[1, s]
        gab = g[:128, 128:]
        u1 = jnp.concatenate([jnp.where(low, gab[:64], 0.0), jnp.where(low, 0.0, gab[64:])], axis=0)
        e = -mm_f32(da, mm_f32(u1, db))
        t01 = jnp.concatenate([da[:64] + roll(e[:64]), roll(db[:64])], axis=0)
        t23 = jnp.concatenate([roll(da[64:]) + e[64:], db[64:]], axis=0)
        u2 = jnp.concatenate(
            [
                jnp.where(low, roll(g[:64, :128]), g[:64, 128:]),
                jnp.where(low, roll(g[128:192, :128]), g[128:192, 128:]),
            ],
            axis=0,
        )
        f = -mm_f32(t01, mm_f32(u2, t23))
        zero = jnp.zeros((64, 128), F32)
        tmat[0:64, 0:128] = da[:64] + jnp.where(low, 0.0, roll(f[:64]))
        tmat[0:64, 128:256] = e[:64] + jnp.where(low, 0.0, f[:64])
        tmat[64:128, 0:128] = da[64:]
        tmat[64:128, 128:256] = e[64:]
        tmat[128:192, 0:128] = jnp.where(low, 0.0, roll(f[64:]))
        tmat[128:192, 128:256] = db[:64] + jnp.where(low, 0.0, f[64:])
        tmat[192:256, 0:128] = zero
        tmat[192:256, 128:256] = db[64:]

    def offset(s):
        return (NU - 1 - s) * (NU - s) // 2

    def outer(k, carry):
        s = NU - k
        sa = s - 1
        z_copy(sa).wait()
        wacc[...] = jnp.zeros_like(wacc)
        s1acc[...] = jnp.zeros_like(s1acc)
        s2acc[...] = jnp.zeros_like(s2acc)
        off_a = offset(sa)
        off_c = off_a - k

        def inner(u, carry):
            i = u - s
            carry = tick(off_a + i, carry)
            do_a(off_a + i, u - 1)
            do_c(off_c + i, u)
            return carry

        carry = lax.fori_loop(s, NU, inner, carry)
        carry = tick(off_a + k, carry)
        do_a(off_a + k, NU - 1)
        merge_t(sa)
        yh, ym, yl = split3(mm_f32(tmat[...], wacc[...]))
        y3[0], y3[1], y3[2] = yh, ym, yl
        return carry

    lax.fori_loop(0, NU, outer, (jnp.int32(0), s0, u0))

    def o_copy(u):
        return pltpu.make_async_copy(xbuf.at[u], out_hbm.at[:, u], o_sem.at[u])

    def final(u, _):
        do_c(NCH - NU + u, u)
        o_copy(u).start()
        return 0

    lax.fori_loop(0, NU, final, 0)
    lax.fori_loop(0, NU, lambda u, _: (o_copy(u).wait(), 0)[1], 0)
    sent = vbuf.at[:, pl.ds(0, 64), pl.ds(0, 128)]
    for k in range(3):
        remote(sent, sent, k, rp_sem.at[0], dev1).wait_send()
    sent = vbuf.at[:, :, pl.ds(0, 128)]
    remote(sent, sent, 3, rp_sem.at[0], devp).wait_send()


def solution(mesh):
    def local_apply(v_loc, t_loc, z_loc):
        t4 = t_loc.reshape(NU, 2, 64, 64)
        zero = jnp.zeros((NU, 64, 64), F32)
        d_loc = jnp.concatenate(
            [jnp.concatenate([t4[:, 0], zero], axis=2), jnp.concatenate([zero, t4[:, 1]], axis=2)], axis=1
        )
        dma = pltpu.SemaphoreType.DMA
        out = pl.pallas_call(
            kernel,
            out_shape=jax.ShapeDtypeStruct((4, NU, 64, 512), F32),
            in_specs=[pl.BlockSpec(memory_space=pl.ANY)] * 3,
            out_specs=pl.BlockSpec(memory_space=pl.ANY),
            scratch_shapes=[
                pltpu.VMEM((NCH, 256, 256), F32),
                pltpu.VMEM((NU, 4, 64, 512), F32),
                pltpu.VMEM((2, NU, 128, 128), F32),
                pltpu.VMEM((3, 256, 256), BF16),
                pltpu.VMEM((3, 256, 256), BF16),
                pltpu.VMEM((3, 256, 512), BF16),
                pltpu.VMEM((3, 256, 512), BF16),
                pltpu.VMEM((256, 512), F32),
                pltpu.VMEM((256, 256), F32),
                pltpu.VMEM((256, 256), F32),
                pltpu.VMEM((256, 256), F32),
                dma((NCH,)), dma((NCH,)), dma((NCH,)), dma((NCH,)), dma((NCH,)),
                dma((4,)), dma((NU,)), dma((3,)), dma((NU,)),
            ],
            compiler_params=pltpu.CompilerParams(
                collective_id=0, has_side_effects=True, vmem_limit_bytes=67_043_328
            ),
            cost_estimate=pl.CostEstimate(flops=116_000_000_000, bytes_accessed=60_000_000, transcendentals=0),
        )(v_loc.reshape(NU, 64, 2048), d_loc, z_loc.reshape(4, NU, 64, 512))
        return out.reshape(4096, 512)

    return jax.shard_map(
        local_apply,
        mesh=mesh,
        in_specs=(P("row", "col"), P("col", None, None), P(None, ("row", "col"))),
        out_specs=P(None, ("row", "col")),
        check_vma=False,
    )
```

time: 3950 us -> 252 us (0.06)
  waiting for transfers between devices: 2260 us -> 0 us
  matrix products: 1330 us -> 0 us
  Pallas kernels: 0 us -> 242 us
  blocking collectives: 236 us -> 0 us
  local copies, waits for them, and re-layouts: 89.6 us -> 9.03 us
    psum x64 -> x0, waiting for transfers between devices: 2170 us -> none  [inner_step(): w_sum = lax.psum(w_part, 'row')]
    dot_general x192 -> x0, matrix products: 1330 us -> none  [the longest x64 695 us: inner_step(): jnp.dot(v_blk, y_blk, precision=FULL_PREC, preferred_element_type=jnp.flo...]
    pallas_call x0 -> x1, Pallas kernels: none -> 242 us  [local_apply(): pl.pallas_call(kernel, out_shape=jax.ShapeDtypeStruct((4, NU, 64, 512), F...]
    all_gather x64 -> x0, blocking collectives: 141 us -> none  [the longest x32 81.9 us: outer_step(): v_all = lax.all_gather(v_own, 'col')]
    all_to_all x1 -> x0, blocking collectives: 95.5 us -> none  [local_apply(): return lax.all_to_all(x_two, 'row', 1, 0, tiled=True)]
    all_to_all x1 -> x0, waiting for transfers between devices: 94 us -> none  [local_apply(): x_two = lax.all_to_all(z_loc, 'row', 0, 1, tiled=True)]
    dynamic_slice x64 -> x0, local copies, waits for them, and re-layouts: 63.9 us -> none  [the longest x32 39.6 us: outer_step(): lax.dynamic_slice_in_dim(v_loc, local_idx * block_w, block_w, axis=1)]
  transfers between devices with their start and end apart: 65 -> 0, of which waited for: 65 -> 0; matrix products, arithmetic and copies ran while one was open for 0% -> 0% of each run, Pallas kernels for 0% -> 0%
where the time goes in v1:
time: 252 us
  Pallas kernels  242 us (96%)
  local copies, waits for them, and re-layouts  9.03 us (4%)
    pallas_call x1, Pallas kernels, local_apply(): pl.pallas_call(kernel, out_shape=jax.ShapeDtypeStruct((4, NU, 64, 512), F...  242 us
    unnamed x1, local copies, waits for them, and re-layouts  7.76 us

profile of v1, /device:TPU:0, one launch (start us, length us, event | category | flops | bytes accessed | tf_op | source)
XLA Modules:
  0.0 252.0 jit_solution(18103674613220113900)
XLA Ops:
  0.0 1.3 slice_bitcast_fusion.1
  1.3 1.2 select_maximum_fusion.d_hbm
  2.5 241.8 %shard_map.37 = f32[4,16,64,512]{3,2,1,0:T(8,128)} custom-call(f32[16,64,2048]{2,1,0:T(8,128)} %bitcast.14, f32[16,128,128]{2,1,0:T(8,128)} %select_maximum_fusion.d_hbm, f32[4,16,64,512]{3,2,1,0:T(8,128)} %bitcast.15), custom_call_target="tpu_custom_call" | custom-call | flops 115999997952 | bytes 60000000 | tf_op jit(solution)/shard_map/pallas_call | solution.py:248
  244.2 7.8 %copy.9 = f32[4096,512]{1,0:T(8,128)} copy(f32[4096,512]{1,0:T(8,128)} %bitcast.12) | data formatting | bytes 16777216

commit v2 on v1

--- a/solution.py
+++ b/solution.py
@@ -37,6 +37,16 @@
 
 def mm_f32(a, b):
     return mm6(split3(a), split3(b))
+
+
+def mm_k128(a, b):
+    ah, am, al = split3(a)
+    bh, bm, bl = split3(b)
+
+    def part(a0, a1, b0, b1):
+        return dot(jnp.concatenate([a0, a1], axis=1), jnp.concatenate([b0, b1], axis=0))
+
+    return (part(am, ah, bm, bl) + part(al, ah, bh, bm)) + part(am, ah, bh, bh)
 
 
 def kernel(
@@ -116,7 +126,11 @@
         n, s, u = carry
         count = jnp.where(c < EXTRA, 2, 1)
         s, u = lax.fori_loop(0, count, lambda i, su: comm_tick(n + i, su), (s, u))
-        stage3(c)
+
+        @pl.when(c < NCH)
+        def _():
+            stage3(c)
+
         return n + count, s, u
 
     barrier = pltpu.get_barrier_semaphore()
@@ -124,7 +138,7 @@
         pl.semaphore_signal(barrier, inc=1, device_id=dev, device_id_type=MESH)
     pl.semaphore_wait(barrier, 3)
 
-    d_own = dbuf.at[q]
+    d_own = dbuf.at[:, :, pl.ds(pl.multiple_of(q * 64, 64), 64), :]
     d_send = pltpu.make_async_remote_copy(
         src_ref=d_hbm, dst_ref=d_own, send_sem=d_sem.at[0], recv_sem=d_sem.at[1],
         device_id=devp, device_id_type=MESH,
@@ -141,24 +155,29 @@
     d_send.wait()
     d_loc.wait()
 
-    def do_a(c, u):
+    def store3(ref, x):
+        ref[0], ref[1], ref[2] = split3(x)
+
+    def load3(ref):
+        return ref[0], ref[1], ref[2]
+
+    def do_a():
+        wacc[...] += mm6(load3(vt3), load3(x3))
+
+    def do_c(c, u):
+        x = xbuf[u].reshape(256, 512) - mm6(split3(vbuf[c]), load3(y3))
+        xbuf[u] = x.reshape(4, 64, 512)
+        return x
+
+    def do_g(c):
         v = vbuf[c]
-        th, tm, tl = split3(v.T)
-        vt3[0], vt3[1], vt3[2] = th, tm, tl
-        nh, nm, nl = split3(v)
-        vn3[0], vn3[1], vn3[2] = nh, nm, nl
-        xh, xm, xl = split3(xbuf[u].reshape(256, 512))
-        x3[0], x3[1], x3[2] = xh, xm, xl
-        wacc[...] += mm6((vt3[0], vt3[1], vt3[2]), (x3[0], x3[1], x3[2]))
-        s1acc[...] += dot(vt3[1], vn3[1]) + dot(vt3[0], vn3[0])
-        s2acc[...] += dot(vt3[0], vn3[2]) + dot(vt3[0], vn3[1])
-
-    def do_c(c, u):
-        upd = mm6(split3(vbuf[c]), (y3[0], y3[1], y3[2]))
-        xbuf[u] = xbuf[u] - upd.reshape(4, 64, 512)
-
-    lane = lax.broadcasted_iota(jnp.int32, (64, 128), 1)
-    low = lane < 64
+        store3(vn3, v)
+        store3(vt3, v.T)
+        g1 = dot(vt3[1], vn3[1]) + dot(vt3[0], vn3[0])
+        g2 = dot(vt3[0], vn3[2]) + dot(vt3[0], vn3[1])
+        return g1, g2
+
+    low = lax.broadcasted_iota(jnp.int32, (64, 128), 1) < 64
 
     def roll(x):
         return pltpu.roll(x, 64, 1)
@@ -166,12 +185,10 @@
     def merge_t(s):
         s2 = s2acc[...]
         g = s1acc[...] + s2 + s2.T
-        da, db = dbuf[0, s], dbuf[1, s]
-        gab = g[:128, 128:]
-        u1 = jnp.concatenate([jnp.where(low, gab[:64], 0.0), jnp.where(low, 0.0, gab[64:])], axis=0)
-        e = -mm_f32(da, mm_f32(u1, db))
-        t01 = jnp.concatenate([da[:64] + roll(e[:64]), roll(db[:64])], axis=0)
-        t23 = jnp.concatenate([roll(da[64:]) + e[64:], db[64:]], axis=0)
+        zero = jnp.zeros((64, 128), F32)
+        d01, d23 = dbuf[s, 0], dbuf[s, 1]
+        u01 = jnp.concatenate([jnp.where(low, 0.0, roll(g[:64, 128:])), zero], axis=0)
+        u23 = jnp.concatenate([jnp.where(low, 0.0, g[64:128, 128:]), zero], axis=0)
         u2 = jnp.concatenate(
             [
                 jnp.where(low, roll(g[:64, :128]), g[:64, 128:]),
@@ -179,46 +196,76 @@
             ],
             axis=0,
         )
-        f = -mm_f32(t01, mm_f32(u2, t23))
-        zero = jnp.zeros((64, 128), F32)
-        tmat[0:64, 0:128] = da[:64] + jnp.where(low, 0.0, roll(f[:64]))
-        tmat[0:64, 128:256] = e[:64] + jnp.where(low, 0.0, f[:64])
-        tmat[64:128, 0:128] = da[64:]
-        tmat[64:128, 128:256] = e[64:]
+        nm = mm_k128(d01, jnp.concatenate([u01, u2], axis=1))
+        z = mm_k128(u23, d23)
+        el = mm_k128(nm[:, :128], jnp.concatenate([d01, nm[:, 128:]], axis=1))
+        t01 = d01 - el[:, :128]
+        t23 = d23 - mm_k128(d23, z)
+        f = -mm_k128(nm[:, 128:] - el[:, 128:], t23)
+        tmat[0:64, 0:128] = jnp.where(low, t01[:64], roll(f[:64]))
+        tmat[0:64, 128:256] = jnp.where(low, roll(t01[:64]), f[:64])
+        tmat[64:128, 0:128] = jnp.where(low, 0.0, roll(t23[:64]))
+        tmat[64:128, 128:256] = jnp.where(low, 0.0, t23[:64])
         tmat[128:192, 0:128] = jnp.where(low, 0.0, roll(f[64:]))
-        tmat[128:192, 128:256] = db[:64] + jnp.where(low, 0.0, f[64:])
+        tmat[128:192, 128:256] = jnp.where(low, roll(t01[64:]), f[64:])
         tmat[192:256, 0:128] = zero
-        tmat[192:256, 128:256] = db[64:]
+        tmat[192:256, 128:256] = t23[64:]
 
     def offset(s):
         return (NU - 1 - s) * (NU - s) // 2
+
+    carry = tick(0, (jnp.int32(0), s0, u0))
+    z_copy(NU - 1).wait()
+    wacc[...] = jnp.zeros_like(wacc)
+    s1acc[...], s2acc[...] = do_g(0)
+    store3(x3, xbuf[NU - 1].reshape(256, 512))
 
     def outer(k, carry):
         s = NU - k
         sa = s - 1
-        z_copy(sa).wait()
-        wacc[...] = jnp.zeros_like(wacc)
-        s1acc[...] = jnp.zeros_like(s1acc)
-        s2acc[...] = jnp.zeros_like(s2acc)
         off_a = offset(sa)
         off_c = off_a - k
 
-        def inner(u, carry):
+        def step(u):
             i = u - s
-            carry = tick(off_a + i, carry)
-            do_a(off_a + i, u - 1)
-            do_c(off_c + i, u)
+            do_a()
+            x = do_c(off_c + i, u)
+            g1, g2 = do_g(off_a + i + 1)
+            s1acc[...] += g1
+            s2acc[...] += g2
+            store3(x3, x)
+
+        def step1(u, carry):
+            carry = tick(off_a + u - s + 1, carry)
+            step(u)
             return carry
 
-        carry = lax.fori_loop(s, NU, inner, carry)
-        carry = tick(off_a + k, carry)
-        do_a(off_a + k, NU - 1)
+        def step2(j, carry):
+            u = s + 2 * j
+            carry = tick(off_a + u - s + 1, carry)
+            carry = tick(off_a + u - s + 2, carry)
+            step(u)
+            step(u + 1)
+            return carry
+
+        carry = lax.fori_loop(0, k // 2, step2, carry)
+        carry = lax.fori_loop(NU - k % 2, NU, step1, carry)
+        more = k < NU - 1
+        carry = tick(off_a + k + 1, carry)
+
+        @pl.when(more)
+        def _():
+            z_copy(jnp.maximum(sa - 1, 0)).wait()
+
+        do_a()
         merge_t(sa)
-        yh, ym, yl = split3(mm_f32(tmat[...], wacc[...]))
-        y3[0], y3[1], y3[2] = yh, ym, yl
+        s1acc[...], s2acc[...] = do_g(jnp.minimum(off_a + k + 1, NCH - 1))
+        store3(x3, xbuf[jnp.maximum(sa - 1, 0)].reshape(256, 512))
+        store3(y3, mm_f32(tmat[...], wacc[...]))
+        wacc[...] = jnp.zeros_like(wacc)
         return carry
 
-    lax.fori_loop(0, NU, outer, (jnp.int32(0), s0, u0))
+    lax.fori_loop(0, NU, outer, carry)
 
     def o_copy(u):
         return pltpu.make_async_copy(xbuf.at[u], out_hbm.at[:, u], o_sem.at[u])
@@ -240,10 +287,9 @@
 def solution(mesh):
     def local_apply(v_loc, t_loc, z_loc):
         t4 = t_loc.reshape(NU, 2, 64, 64)
-        zero = jnp.zeros((NU, 64, 64), F32)
-        d_loc = jnp.concatenate(
-            [jnp.concatenate([t4[:, 0], zero], axis=2), jnp.concatenate([zero, t4[:, 1]], axis=2)], axis=1
-        )
+        zero = jnp.zeros_like(t4)
+        first = lax.axis_index("col") == 0
+        d_loc = jnp.concatenate([jnp.where(first, t4, zero), jnp.where(first, zero, t4)], axis=3)
         dma = pltpu.SemaphoreType.DMA
         out = pl.pallas_call(
             kernel,
@@ -253,7 +299,7 @@
             scratch_shapes=[
                 pltpu.VMEM((NCH, 256, 256), F32),
                 pltpu.VMEM((NU, 4, 64, 512), F32),
-                pltpu.VMEM((2, NU, 128, 128), F32),
+                pltpu.VMEM((NU, 2, 128, 128), F32),
                 pltpu.VMEM((3, 256, 256), BF16),
                 pltpu.VMEM((3, 256, 256), BF16),
                 pltpu.VMEM((3, 256, 512), BF16),

time: 252 us -> 232 us (0.921)
  Pallas kernels: 242 us -> 221 us
    pallas_call x1, Pallas kernels: 242 us -> 221 us  [local_apply(): pl.pallas_call(kernel, out_shape=jax.ShapeDtypeStruct((4, NU, 64, 512), F...]
where the time goes in v2:
time: 232 us
  Pallas kernels  221 us (95%)
  local copies, waits for them, and re-layouts  7.76 us (3%)
  other arithmetic  2.78 us (1%)
    pallas_call x1, Pallas kernels, local_apply(): pl.pallas_call(kernel, out_shape=jax.ShapeDtypeStruct((4, NU, 64, 512), F...  221 us
    unnamed x1, local copies, waits for them, and re-layouts  7.76 us

profile of v2, /device:TPU:0, one launch (start us, length us, event | category | flops | bytes accessed | tf_op | source)
XLA Modules:
  0.0 231.9 jit_solution(6991595693486806024)
XLA Ops:
  0.0 1.5 broadcast_select_fusion.1
  1.5 1.3 pad_maximum_fusion.d_hbm
  2.8 221.3 %shard_map.37 = f32[4,16,64,512]{3,2,1,0:T(8,128)} custom-call(f32[16,64,2048]{2,1,0:T(8,128)} %bitcast.8, f32[16,2,64,128]{3,2,1,0:T(8,128)} %pad_maximum_fusion.d_hbm, f32[4,16,64,512]{3,2,1,0:T(8,128)} %bitcast.9), custom_call_target="tpu_custom_call" | custom-call | flops 115999997952 | bytes 60000000 | tf_op jit(solution)/shard_map/pallas_call | solution.py:294
  224.1 7.8 %copy.5 = f32[4096,512]{1,0:T(8,128)} copy(f32[4096,512]{1,0:T(8,128)} %bitcast.5) | data formatting | bytes 16777216

commit v3 on v2

--- a/solution.py
+++ b/solution.py
@@ -13,8 +13,8 @@
 
 NU = 16
 NCH = NU * (NU + 1) // 2
-L0, L1, L2 = 12, 7, 3
-EXTRA = 24
+LEAD0, LEAD1, LEAD2 = 9, 3, 1
+ZAHEAD = 4
 
 
 def split3(x):
@@ -102,36 +102,50 @@
         p = vbuf.at[c, :, pl.ds(pl.multiple_of((1 - q) * 128, 128), 128)]
         remote(p, p, 3, rp_sem.at[c], devp).wait_recv()
 
-    def comm_tick(n, su):
-        s, u = su
-
-        @pl.when(n + L0 < NCH)
-        def _():
-            stage0(n + L0, s, u)
-
-        @pl.when(jnp.logical_and(n + L1 >= 0, n + L1 < NCH))
-        def _():
-            stage1(n + L1)
-
-        @pl.when(jnp.logical_and(n + L2 >= 0, n + L2 < NCH))
-        def _():
-            stage2(n + L2)
+    def next0(carry):
+        n0, s, u, n1, n2 = carry
+
+        @pl.when(n0 < NCH)
+        def _():
+            stage0(n0, s, u)
 
         last = u == NU - 1
         s2 = jnp.where(last, jnp.maximum(s - 1, 0), s)
         u2 = jnp.where(last, s2, u + 1)
-        return s2, u2
+        return n0 + 1, s2, u2, n1, n2
+
+    def next1(carry):
+        n0, s, u, n1, n2 = carry
+
+        @pl.when(n1 < NCH)
+        def _():
+            stage1(n1)
+
+        return n0, s, u, n1 + 1, n2
+
+    def next2(carry):
+        n0, s, u, n1, n2 = carry
+
+        @pl.when(n2 < NCH)
+        def _():
+            stage2(n2)
+
+        return n0, s, u, n1, n2 + 1
+
+    def repeat(count, fn, carry):
+        return lax.fori_loop(0, count, lambda i, c: fn(c), carry)
+
+    def advance(carry):
+        return next2(next1(next0(carry)))
 
     def tick(c, carry):
-        n, s, u = carry
-        count = jnp.where(c < EXTRA, 2, 1)
-        s, u = lax.fori_loop(0, count, lambda i, su: comm_tick(n + i, su), (s, u))
+        carry = advance(carry)
 
         @pl.when(c < NCH)
         def _():
             stage3(c)
 
-        return n + count, s, u
+        return carry
 
     barrier = pltpu.get_barrier_semaphore()
     for dev in (dev1, dev2, devp):
@@ -150,8 +164,13 @@
     def z_copy(u):
         return pltpu.make_async_copy(z_hbm.at[:, u], xbuf.at[u], z_sem.at[u])
 
-    s0, u0 = lax.fori_loop(-L0, 0, comm_tick, (jnp.int32(NU - 1), jnp.int32(NU - 1)))
-    lax.fori_loop(0, NU, lambda i, _: (z_copy(NU - 1 - i).start(), 0)[1], 0)
+    for i in range(ZAHEAD):
+        z_copy(NU - 1 - i).start()
+    zero = jnp.int32(0)
+    carry = (zero, jnp.int32(NU - 1), jnp.int32(NU - 1), zero, zero)
+    carry = repeat(LEAD0, next0, carry)
+    carry = repeat(LEAD1, next1, carry)
+    carry = repeat(LEAD2, next2, carry)
     d_send.wait()
     d_loc.wait()
 
@@ -214,7 +233,7 @@
     def offset(s):
         return (NU - 1 - s) * (NU - s) // 2
 
-    carry = tick(0, (jnp.int32(0), s0, u0))
+    carry = tick(0, carry)
     z_copy(NU - 1).wait()
     wacc[...] = jnp.zeros_like(wacc)
     s1acc[...], s2acc[...] = do_g(0)
@@ -250,12 +269,16 @@
 
         carry = lax.fori_loop(0, k // 2, step2, carry)
         carry = lax.fori_loop(NU - k % 2, NU, step1, carry)
-        more = k < NU - 1
+        carry = repeat(k % 2, advance, carry)
         carry = tick(off_a + k + 1, carry)
 
-        @pl.when(more)
-        def _():
-            z_copy(jnp.maximum(sa - 1, 0)).wait()
+        @pl.when(sa >= ZAHEAD)
+        def _():
+            z_copy(sa - ZAHEAD).start()
+
+        @pl.when(sa >= 1)
+        def _():
+            z_copy(sa - 1).wait()
 
         do_a()
         merge_t(sa)

time: 232 us -> 272 us (1.17)
  Pallas kernels: 221 us -> 261 us
    pallas_call x1, Pallas kernels: 221 us -> 261 us  [local_apply(): pl.pallas_call(kernel, out_shape=jax.ShapeDtypeStruct((4, NU, 64, 512), F...]
where the time goes in v3:
time: 272 us
  Pallas kernels  261 us (96%)
  local copies, waits for them, and re-layouts  7.76 us (3%)
  other arithmetic  2.78 us (1%)
    pallas_call x1, Pallas kernels, local_apply(): pl.pallas_call(kernel, out_shape=jax.ShapeDtypeStruct((4, NU, 64, 512), F...  261 us
    unnamed x1, local copies, waits for them, and re-layouts  7.76 us

profile of v3, /device:TPU:0, one launch (start us, length us, event | category | flops | bytes accessed | tf_op | source)
XLA Modules:
  0.0 271.9 jit_solution(15880901768428860836)
XLA Ops:
  0.0 1.5 broadcast_select_fusion.1
  1.5 1.3 pad_maximum_fusion.d_hbm
  2.8 261.3 %shard_map.37 = f32[4,16,64,512]{3,2,1,0:T(8,128)} custom-call(f32[16,64,2048]{2,1,0:T(8,128)} %bitcast.8, f32[16,2,64,128]{3,2,1,0:T(8,128)} %pad_maximum_fusion.d_hbm, f32[4,16,64,512]{3,2,1,0:T(8,128)} %bitcast.9), custom_call_target="tpu_custom_call" | custom-call | flops 115999997952 | bytes 60000000 | tf_op jit(solution)/shard_map/pallas_call | solution.py:317
  264.1 7.8 %copy.5 = f32[4096,512]{1,0:T(8,128)} copy(f32[4096,512]{1,0:T(8,128)} %bitcast.5) | data formatting | bytes 16777216

commit v4 on v3

--- a/solution.py
+++ b/solution.py
@@ -13,7 +13,7 @@
 
 NU = 16
 NCH = NU * (NU + 1) // 2
-LEAD0, LEAD1, LEAD2 = 9, 3, 1
+LEAD, GROW, LEAD_MAX = (8, 4, 1), (12, 8, 16), (14, 8, 2)
 ZAHEAD = 4
 
 
@@ -102,50 +102,37 @@
         p = vbuf.at[c, :, pl.ds(pl.multiple_of((1 - q) * 128, 128), 128)]
         remote(p, p, 3, rp_sem.at[c], devp).wait_recv()
 
-    def next0(carry):
-        n0, s, u, n1, n2 = carry
-
-        @pl.when(n0 < NCH)
-        def _():
-            stage0(n0, s, u)
-
-        last = u == NU - 1
-        s2 = jnp.where(last, jnp.maximum(s - 1, 0), s)
-        u2 = jnp.where(last, s2, u + 1)
-        return n0 + 1, s2, u2, n1, n2
-
-    def next1(carry):
-        n0, s, u, n1, n2 = carry
-
-        @pl.when(n1 < NCH)
-        def _():
-            stage1(n1)
-
-        return n0, s, u, n1 + 1, n2
-
-    def next2(carry):
-        n0, s, u, n1, n2 = carry
-
-        @pl.when(n2 < NCH)
-        def _():
-            stage2(n2)
-
-        return n0, s, u, n1, n2 + 1
-
-    def repeat(count, fn, carry):
-        return lax.fori_loop(0, count, lambda i, c: fn(c), carry)
-
-    def advance(carry):
-        return next2(next1(next0(carry)))
-
-    def tick(c, carry):
-        carry = advance(carry)
+    def target(i, c):
+        ahead = jnp.minimum(LEAD[i] + c * GROW[i] // 16, LEAD_MAX[i])
+        return jnp.minimum(c + ahead, NCH)
+
+    def run0(lo, hi, su):
+        def body(n, su):
+            s, u = su
+            stage0(n, s, u)
+            last = u == NU - 1
+            s2 = jnp.where(last, jnp.maximum(s - 1, 0), s)
+            return s2, jnp.where(last, s2, u + 1)
+
+        return lax.fori_loop(lo, hi, body, su)
+
+    def run(i, lo, hi):
+        def body(n, _):
+            (None, stage1, stage2)[i](n)
+            return 0
+
+        lax.fori_loop(lo, hi, body, 0)
+
+    def tick(c, su):
+        for i in (1, 2):
+            run(i, target(i, c), target(i, c + 1))
+        su = run0(target(0, c), target(0, c + 1), su)
 
         @pl.when(c < NCH)
         def _():
             stage3(c)
 
-        return carry
+        return su
 
     barrier = pltpu.get_barrier_semaphore()
     for dev in (dev1, dev2, devp):
@@ -166,11 +153,9 @@
 
     for i in range(ZAHEAD):
         z_copy(NU - 1 - i).start()
-    zero = jnp.int32(0)
-    carry = (zero, jnp.int32(NU - 1), jnp.int32(NU - 1), zero, zero)
-    carry = repeat(LEAD0, next0, carry)
-    carry = repeat(LEAD1, next1, carry)
-    carry = repeat(LEAD2, next2, carry)
+    carry = run0(0, target(0, 0), (jnp.int32(NU - 1), jnp.int32(NU - 1)))
+    for i in (1, 2):
+        run(i, 0, target(i, 0))
     d_send.wait()
     d_loc.wait()
 
@@ -269,7 +254,6 @@
 
         carry = lax.fori_loop(0, k // 2, step2, carry)
         carry = lax.fori_loop(NU - k % 2, NU, step1, carry)
-        carry = repeat(k % 2, advance, carry)
         carry = tick(off_a + k + 1, carry)
 
         @pl.when(sa >= ZAHEAD)

time: 272 us -> 213 us (0.78)
  Pallas kernels: 261 us -> 202 us
    pallas_call x1, Pallas kernels: 261 us -> 202 us  [local_apply(): pl.pallas_call(kernel, out_shape=jax.ShapeDtypeStruct((4, NU, 64, 512), F...]
where the time goes in v4:
time: 213 us
  Pallas kernels  202 us (95%)
  local copies, waits for them, and re-layouts  7.76 us (4%)
  other arithmetic  2.78 us (1%)
    pallas_call x1, Pallas kernels, local_apply(): pl.pallas_call(kernel, out_shape=jax.ShapeDtypeStruct((4, NU, 64, 512), F...  202 us
    unnamed x1, local copies, waits for them, and re-layouts  7.76 us

profile of v4, /device:TPU:0, one launch (start us, length us, event | category | flops | bytes accessed | tf_op | source)
XLA Modules:
  0.0 212.6 jit_solution(7919673930523195695)
XLA Ops:
  0.0 1.5 broadcast_select_fusion.1
  1.5 1.3 pad_maximum_fusion.d_hbm
  2.8 202.0 %shard_map.37 = f32[4,16,64,512]{3,2,1,0:T(8,128)} custom-call(f32[16,64,2048]{2,1,0:T(8,128)} %bitcast.8, f32[16,2,64,128]{3,2,1,0:T(8,128)} %pad_maximum_fusion.d_hbm, f32[4,16,64,512]{3,2,1,0:T(8,128)} %bitcast.9), custom_call_target="tpu_custom_call" | custom-call | flops 115999997952 | bytes 60000000 | tf_op jit(solution)/shard_map/pallas_call | solution.py:301
  204.8 7.8 %copy.5 = f32[4096,512]{1,0:T(8,128)} copy(f32[4096,512]{1,0:T(8,128)} %bitcast.5) | data formatting | bytes 16777216

commit v5 on v4

--- a/solution.py
+++ b/solution.py
@@ -51,7 +51,7 @@
 
 def kernel(
     v_hbm, d_hbm, z_hbm, out_hbm,
-    vbuf, xbuf, dbuf, vt3, vn3, x3, y3, wacc, s1acc, s2acc, tmat,
+    vbuf, xbuf, dbuf, vt3, vt3b, vn3, x3, x3b, y3, wacc, s1acc, s2acc, tmat,
     r1_sem, r2_sem, rd_sem, rp_sem, loc_sem, send_sem, z_sem, d_sem, o_sem,
 ):
     r = lax.axis_index("row")
@@ -165,20 +165,20 @@
     def load3(ref):
         return ref[0], ref[1], ref[2]
 
-    def do_a():
-        wacc[...] += mm6(load3(vt3), load3(x3))
+    def do_a(vt, x):
+        return mm6(load3(vt), load3(x))
 
     def do_c(c, u):
         x = xbuf[u].reshape(256, 512) - mm6(split3(vbuf[c]), load3(y3))
         xbuf[u] = x.reshape(4, 64, 512)
         return x
 
-    def do_g(c):
+    def do_g(c, vt):
         v = vbuf[c]
         store3(vn3, v)
-        store3(vt3, v.T)
-        g1 = dot(vt3[1], vn3[1]) + dot(vt3[0], vn3[0])
-        g2 = dot(vt3[0], vn3[2]) + dot(vt3[0], vn3[1])
+        store3(vt, v.T)
+        g1 = dot(vt[1], vn3[1]) + dot(vt[0], vn3[0])
+        g2 = dot(vt[0], vn3[2]) + dot(vt[0], vn3[1])
         return g1, g2
 
     low = lax.broadcasted_iota(jnp.int32, (64, 128), 1) < 64
@@ -186,9 +186,8 @@
     def roll(x):
         return pltpu.roll(x, 64, 1)
 
-    def merge_t(s):
-        s2 = s2acc[...]
-        g = s1acc[...] + s2 + s2.T
+    def merge_1(s, s1, s2):
+        g = s1 + s2 + s2.T
         zero = jnp.zeros((64, 128), F32)
         d01, d23 = dbuf[s, 0], dbuf[s, 1]
         u01 = jnp.concatenate([jnp.where(low, 0.0, roll(g[:64, 128:])), zero], axis=0)
@@ -202,17 +201,23 @@
         )
         nm = mm_k128(d01, jnp.concatenate([u01, u2], axis=1))
         z = mm_k128(u23, d23)
+        return nm, z
+
+    def merge_2(s, nm, z):
+        d01, d23 = dbuf[s, 0], dbuf[s, 1]
         el = mm_k128(nm[:, :128], jnp.concatenate([d01, nm[:, 128:]], axis=1))
-        t01 = d01 - el[:, :128]
         t23 = d23 - mm_k128(d23, z)
-        f = -mm_k128(nm[:, 128:] - el[:, 128:], t23)
+        return d01 - el[:, :128], nm[:, 128:] - el[:, 128:], t23
+
+    def merge_3(t01, lm, t23):
+        f = -mm_k128(lm, t23)
         tmat[0:64, 0:128] = jnp.where(low, t01[:64], roll(f[:64]))
         tmat[0:64, 128:256] = jnp.where(low, roll(t01[:64]), f[:64])
         tmat[64:128, 0:128] = jnp.where(low, 0.0, roll(t23[:64]))
         tmat[64:128, 128:256] = jnp.where(low, 0.0, t23[:64])
         tmat[128:192, 0:128] = jnp.where(low, 0.0, roll(f[64:]))
         tmat[128:192, 128:256] = jnp.where(low, roll(t01[64:]), f[64:])
-        tmat[192:256, 0:128] = zero
+        tmat[192:256, 0:128] = jnp.zeros((64, 128), F32)
         tmat[192:256, 128:256] = t23[64:]
 
     def offset(s):
@@ -221,8 +226,41 @@
     carry = tick(0, carry)
     z_copy(NU - 1).wait()
     wacc[...] = jnp.zeros_like(wacc)
-    s1acc[...], s2acc[...] = do_g(0)
+    s1acc[...], s2acc[...] = do_g(0, vt3)
     store3(x3, xbuf[NU - 1].reshape(256, 512))
+
+    def step(c_a, c_c, u):
+        wacc[...] += do_a(vt3, x3)
+        x = do_c(c_c, u)
+        g1, g2 = do_g(c_a + 1, vt3)
+        s1acc[...] += g1
+        s2acc[...] += g2
+        store3(x3, x)
+
+    def first_g(c):
+        s1acc[...], s2acc[...] = do_g(jnp.minimum(c, NCH - 1), vt3)
+
+    def finish(sa, w):
+        store3(x3, xbuf[jnp.maximum(sa - 1, 0)].reshape(256, 512))
+        store3(y3, mm_f32(tmat[...], w))
+        wacc[...] = jnp.zeros_like(wacc)
+
+    def next_z(sa):
+        @pl.when(sa >= ZAHEAD)
+        def _():
+            z_copy(sa - ZAHEAD).start()
+
+        @pl.when(sa >= 1)
+        def _():
+            z_copy(sa - 1).wait()
+
+    carry = tick(1, carry)
+    next_z(NU - 1)
+    vt3b[...] = vt3[...]
+    x3b[...] = x3[...]
+    merge_3(*merge_2(NU - 1, *merge_1(NU - 1, s1acc[...], s2acc[...])))
+    first_g(1)
+    finish(NU - 1, do_a(vt3b, x3b))
 
     def outer(k, carry):
         s = NU - k
@@ -230,49 +268,39 @@
         off_a = offset(sa)
         off_c = off_a - k
 
-        def step(u):
+        def step1(u, carry):
             i = u - s
-            do_a()
-            x = do_c(off_c + i, u)
-            g1, g2 = do_g(off_a + i + 1)
-            s1acc[...] += g1
-            s2acc[...] += g2
-            store3(x3, x)
-
-        def step1(u, carry):
-            carry = tick(off_a + u - s + 1, carry)
-            step(u)
+            carry = tick(off_a + i + 1, carry)
+            step(off_a + i, off_c + i, u)
             return carry
 
         def step2(j, carry):
-            u = s + 2 * j
-            carry = tick(off_a + u - s + 1, carry)
-            carry = tick(off_a + u - s + 2, carry)
-            step(u)
-            step(u + 1)
+            i = 2 * j
+            carry = tick(off_a + i + 1, carry)
+            carry = tick(off_a + i + 2, carry)
+            step(off_a + i, off_c + i, s + i)
+            step(off_a + i + 1, off_c + i + 1, s + i + 1)
             return carry
 
-        carry = lax.fori_loop(0, k // 2, step2, carry)
-        carry = lax.fori_loop(NU - k % 2, NU, step1, carry)
+        pairs = (k - 1) // 2
+        carry = lax.fori_loop(0, pairs, step2, carry)
+        carry = lax.fori_loop(s + 2 * pairs, NU - 1, step1, carry)
+
+        carry = tick(off_a + k, carry)
         carry = tick(off_a + k + 1, carry)
-
-        @pl.when(sa >= ZAHEAD)
-        def _():
-            z_copy(sa - ZAHEAD).start()
-
-        @pl.when(sa >= 1)
-        def _():
-            z_copy(sa - 1).wait()
-
-        do_a()
-        merge_t(sa)
-        s1acc[...], s2acc[...] = do_g(jnp.minimum(off_a + k + 1, NCH - 1))
-        store3(x3, xbuf[jnp.maximum(sa - 1, 0)].reshape(256, 512))
-        store3(y3, mm_f32(tmat[...], wacc[...]))
-        wacc[...] = jnp.zeros_like(wacc)
+        next_z(sa)
+        store3(x3b, do_c(off_c + k - 1, NU - 1))
+        g1, g2 = do_g(off_a + k, vt3b)
+        w = wacc[...] + do_a(vt3, x3)
+        part = merge_1(sa, s1acc[...] + g1, s2acc[...] + g2)
+        w = w + do_a(vt3b, x3b)
+        part = merge_2(sa, *part)
+        first_g(off_a + k + 1)
+        merge_3(*part)
+        finish(sa, w)
         return carry
 
-    lax.fori_loop(0, NU, outer, carry)
+    lax.fori_loop(1, NU, outer, carry)
 
     def o_copy(u):
         return pltpu.make_async_copy(xbuf.at[u], out_hbm.at[:, u], o_sem.at[u])
@@ -309,6 +337,8 @@
                 pltpu.VMEM((NU, 2, 128, 128), F32),
                 pltpu.VMEM((3, 256, 256), BF16),
                 pltpu.VMEM((3, 256, 256), BF16),
+                pltpu.VMEM((3, 256, 256), BF16),
+                pltpu.VMEM((3, 256, 512), BF16),
                 pltpu.VMEM((3, 256, 512), BF16),
                 pltpu.VMEM((3, 256, 512), BF16),
                 pltpu.VMEM((256, 512), F32),

time: 213 us -> 209 us (0.981)
  Pallas kernels: 202 us -> 198 us
    pallas_call x1, Pallas kernels: 202 us -> 198 us  [local_apply(): pl.pallas_call(kernel, out_shape=jax.ShapeDtypeStruct((4, NU, 64, 512), F...]
where the time goes in v5:
time: 209 us; the launch traced here: 208 us
  Pallas kernels  198 us (95%)
  local copies, waits for them, and re-layouts  7.76 us (4%)
  other arithmetic  2.78 us (1%)
    pallas_call x1, Pallas kernels, local_apply(): pl.pallas_call(kernel, out_shape=jax.ShapeDtypeStruct((4, NU, 64, 512), F...  198 us
    unnamed x1, local copies, waits for them, and re-layouts  7.76 us

profile of v5, /device:TPU:0, one launch (start us, length us, event | category | flops | bytes accessed | tf_op | source)
XLA Modules:
  0.0 208.4 jit_solution(6736763503813193174)
XLA Ops:
  0.0 1.5 broadcast_select_fusion.1
  1.5 1.3 pad_maximum_fusion.d_hbm
  2.8 197.8 %shard_map.37 = f32[4,16,64,512]{3,2,1,0:T(8,128)} custom-call(f32[16,64,2048]{2,1,0:T(8,128)} %bitcast.8, f32[16,2,64,128]{3,2,1,0:T(8,128)} %pad_maximum_fusion.d_hbm, f32[4,16,64,512]{3,2,1,0:T(8,128)} %bitcast.9), custom_call_target="tpu_custom_call" | custom-call | flops 115999997952 | bytes 60000000 | tf_op jit(solution)/shard_map/pallas_call | solution.py:329
  200.6 7.8 %copy.5 = f32[4096,512]{1,0:T(8,128)} copy(f32[4096,512]{1,0:T(8,128)} %bitcast.5) | data formatting | bytes 16777216

commit v6 on v5

--- a/solution.py
+++ b/solution.py
@@ -13,7 +13,8 @@
 
 NU = 16
 NCH = NU * (NU + 1) // 2
-LEAD, GROW, LEAD_MAX = (8, 4, 1), (12, 8, 16), (14, 8, 2)
+NP = NCH // 2
+LEAD, GROW, LEAD_MAX = (5, 3, 1), (4, 2, 8), (9, 5, 1)
 ZAHEAD = 4
 
 
@@ -52,7 +53,7 @@
 def kernel(
     v_hbm, d_hbm, z_hbm, out_hbm,
     vbuf, xbuf, dbuf, vt3, vt3b, vn3, x3, x3b, y3, wacc, s1acc, s2acc, tmat,
-    r1_sem, r2_sem, rd_sem, rp_sem, loc_sem, send_sem, z_sem, d_sem, o_sem,
+    r1_sem, r2_sem, rp_sem, send_sem, z_sem, d_sem, o_sem,
 ):
     r = lax.axis_index("row")
     q = lax.axis_index("col")
@@ -61,12 +62,11 @@
     row_y = (1 - ry) * 2 + rx
     n1 = row_x * (1 - q) + row_y * q
     n2 = row_y * (1 - q) + row_x * q
-    nd = 3 - r
     dev1, dev2, devp = (n1, q), (n2, q), (r, 1 - q)
     cols = pl.ds(pl.multiple_of(q * 128, 128), 128)
 
-    def piece(c, rr):
-        return vbuf.at[c, pl.ds(pl.multiple_of(rr * 64, 64), 64), cols]
+    def piece(c, n, rr):
+        return vbuf.at[pl.ds(c, n), pl.ds(pl.multiple_of(rr * 64, 64), 64), cols]
 
     def remote(src, dst, k, rsem, dev):
         return pltpu.make_async_remote_copy(
@@ -74,45 +74,41 @@
             device_id=dev, device_id_type=MESH,
         )
 
-    def own_src(s, u):
-        return v_hbm.at[u, :, pl.ds(pl.multiple_of(s * 128, 128), 128)]
-
-    def stage0(c, s, u):
-        src = own_src(s, u)
-        remote(src, piece(c, r), 0, r1_sem.at[c], dev1).start()
-        remote(src, piece(c, r), 1, r2_sem.at[c], dev2).start()
-        pltpu.make_async_copy(src, piece(c, r), loc_sem.at[c]).start()
-
-    def stage1(c):
-        p = piece(c, n1)
-        remote(p, p, 0, r1_sem.at[c], dev1).wait_recv()
-        remote(p, p, 2, rd_sem.at[c], dev2).start()
-
-    def stage2(c):
-        p = piece(c, n2)
-        remote(p, p, 1, r2_sem.at[c], dev2).wait_recv()
-        p = piece(c, nd)
-        remote(p, p, 2, rd_sem.at[c], dev2).wait_recv()
-        p = piece(c, r)
-        pltpu.make_async_copy(p, p, loc_sem.at[c]).wait()
-        p = vbuf.at[c, :, cols]
-        remote(p, p, 3, rp_sem.at[c], devp).start()
-
-    def stage3(c):
-        p = vbuf.at[c, :, pl.ds(pl.multiple_of((1 - q) * 128, 128), 128)]
-        remote(p, p, 3, rp_sem.at[c], devp).wait_recv()
-
-    def target(i, c):
-        ahead = jnp.minimum(LEAD[i] + c * GROW[i] // 16, LEAD_MAX[i])
-        return jnp.minimum(c + ahead, NCH)
+    def stage0(p, c, s, u):
+        src = v_hbm.at[pl.ds(u, 1), :, pl.ds(pl.multiple_of(s * 128, 128), 128)]
+        dst = piece(c, 1, r)
+        remote(src, dst, 0, r1_sem.at[p], dev1).start()
+        remote(src, dst, 1, r2_sem.at[p], dev2).start()
+        pltpu.make_async_copy(src, dst, r2_sem.at[p]).start()
+
+    def stage1(p):
+        x = piece(2 * p, 2, n1)
+        remote(x, x, 0, r1_sem.at[p], dev1).wait_recv()
+        remote(x, x, 2, r2_sem.at[p], dev2).start()
+
+    def stage2(p):
+        x = vbuf.at[pl.ds(2 * p, 2), pl.ds(0, 192), cols]
+        remote(x, x, 1, r2_sem.at[p], dev2).wait_recv()
+        x = vbuf.at[pl.ds(2 * p, 2), :, cols]
+        remote(x, x, 3, rp_sem.at[p], devp).start()
+
+    def stage3(p):
+        x = vbuf.at[pl.ds(2 * p, 2), :, pl.ds(pl.multiple_of((1 - q) * 128, 128), 128)]
+        remote(x, x, 3, rp_sem.at[p], devp).wait_recv()
+
+    def target(i, p):
+        ahead = jnp.minimum(LEAD[i] + p * GROW[i] // 16, LEAD_MAX[i])
+        return jnp.minimum(p + ahead, NP)
 
     def run0(lo, hi, su):
-        def body(n, su):
+        def body(p, su):
             s, u = su
-            stage0(n, s, u)
-            last = u == NU - 1
-            s2 = jnp.where(last, jnp.maximum(s - 1, 0), s)
-            return s2, jnp.where(last, s2, u + 1)
+            for i in range(2):
+                stage0(p, 2 * p + i, s, u)
+                last = u == NU - 1
+                s2 = jnp.where(last, jnp.maximum(s - 1, 0), s)
+                s, u = s2, jnp.where(last, s2, u + 1)
+            return s, u
 
         return lax.fori_loop(lo, hi, body, su)
 
@@ -123,14 +119,14 @@
 
         lax.fori_loop(lo, hi, body, 0)
 
-    def tick(c, su):
+    def tick(p, su):
         for i in (1, 2):
-            run(i, target(i, c), target(i, c + 1))
-        su = run0(target(0, c), target(0, c + 1), su)
-
-        @pl.when(c < NCH)
+            run(i, target(i, p), target(i, p + 1))
+        su = run0(target(0, p), target(0, p + 1), su)
+
+        @pl.when(p < NP)
         def _():
-            stage3(c)
+            stage3(p)
 
         return su
 
@@ -139,7 +135,7 @@
         pl.semaphore_signal(barrier, inc=1, device_id=dev, device_id_type=MESH)
     pl.semaphore_wait(barrier, 3)
 
-    d_own = dbuf.at[:, :, pl.ds(pl.multiple_of(q * 64, 64), 64), :]
+    d_own = dbuf.at[q]
     d_send = pltpu.make_async_remote_copy(
         src_ref=d_hbm, dst_ref=d_own, send_sem=d_sem.at[0], recv_sem=d_sem.at[1],
         device_id=devp, device_id_type=MESH,
@@ -186,10 +182,20 @@
     def roll(x):
         return pltpu.roll(x, 64, 1)
 
+    def diag(s, i):
+        zero = jnp.zeros((64, 64), F32)
+        return jnp.concatenate(
+            [
+                jnp.concatenate([dbuf[0, s, i], zero], axis=1),
+                jnp.concatenate([zero, dbuf[1, s, i]], axis=1),
+            ],
+            axis=0,
+        )
+
     def merge_1(s, s1, s2):
         g = s1 + s2 + s2.T
         zero = jnp.zeros((64, 128), F32)
-        d01, d23 = dbuf[s, 0], dbuf[s, 1]
+        d01, d23 = diag(s, 0), diag(s, 1)
         u01 = jnp.concatenate([jnp.where(low, 0.0, roll(g[:64, 128:])), zero], axis=0)
         u23 = jnp.concatenate([jnp.where(low, 0.0, g[64:128, 128:]), zero], axis=0)
         u2 = jnp.concatenate(
@@ -204,7 +210,7 @@
         return nm, z
 
     def merge_2(s, nm, z):
-        d01, d23 = dbuf[s, 0], dbuf[s, 1]
+        d01, d23 = diag(s, 0), diag(s, 1)
         el = mm_k128(nm[:, :128], jnp.concatenate([d01, nm[:, 128:]], axis=1))
         t23 = d23 - mm_k128(d23, z)
         return d01 - el[:, :128], nm[:, 128:] - el[:, 128:], t23
@@ -254,7 +260,6 @@
         def _():
             z_copy(sa - 1).wait()
 
-    carry = tick(1, carry)
     next_z(NU - 1)
     vt3b[...] = vt3[...]
     x3b[...] = x3[...]
@@ -270,14 +275,14 @@
 
         def step1(u, carry):
             i = u - s
-            carry = tick(off_a + i + 1, carry)
+            c = off_a + i + 1
+            carry = lax.cond(c % 2 == 0, lambda su: tick(c // 2, su), lambda su: su, carry)
             step(off_a + i, off_c + i, u)
             return carry
 
         def step2(j, carry):
             i = 2 * j
-            carry = tick(off_a + i + 1, carry)
-            carry = tick(off_a + i + 2, carry)
+            carry = tick((off_a + i + 2) // 2, carry)
             step(off_a + i, off_c + i, s + i)
             step(off_a + i + 1, off_c + i + 1, s + i + 1)
             return carry
@@ -286,8 +291,7 @@
         carry = lax.fori_loop(0, pairs, step2, carry)
         carry = lax.fori_loop(s + 2 * pairs, NU - 1, step1, carry)
 
-        carry = tick(off_a + k, carry)
-        carry = tick(off_a + k + 1, carry)
+        carry = tick((off_a + k + 1) // 2, carry)
         next_z(sa)
         store3(x3b, do_c(off_c + k - 1, NU - 1))
         g1, g2 = do_g(off_a + k, vt3b)
@@ -321,10 +325,6 @@
 
 def solution(mesh):
     def local_apply(v_loc, t_loc, z_loc):
-        t4 = t_loc.reshape(NU, 2, 64, 64)
-        zero = jnp.zeros_like(t4)
-        first = lax.axis_index("col") == 0
-        d_loc = jnp.concatenate([jnp.where(first, t4, zero), jnp.where(first, zero, t4)], axis=3)
         dma = pltpu.SemaphoreType.DMA
         out = pl.pallas_call(
             kernel,
@@ -334,7 +334,7 @@
             scratch_shapes=[
                 pltpu.VMEM((NCH, 256, 256), F32),
                 pltpu.VMEM((NU, 4, 64, 512), F32),
-                pltpu.VMEM((NU, 2, 128, 128), F32),
+                pltpu.VMEM((2, NU, 2, 64, 64), F32),
                 pltpu.VMEM((3, 256, 256), BF16),
                 pltpu.VMEM((3, 256, 256), BF16),
                 pltpu.VMEM((3, 256, 256), BF16),
@@ -345,14 +345,14 @@
                 pltpu.VMEM((256, 256), F32),
                 pltpu.VMEM((256, 256), F32),
                 pltpu.VMEM((256, 256), F32),
-                dma((NCH,)), dma((NCH,)), dma((NCH,)), dma((NCH,)), dma((NCH,)),
+                dma((NP,)), dma((NP,)), dma((NP,)),
                 dma((4,)), dma((NU,)), dma((3,)), dma((NU,)),
             ],
             compiler_params=pltpu.CompilerParams(
                 collective_id=0, has_side_effects=True, vmem_limit_bytes=67_043_328
             ),
             cost_estimate=pl.CostEstimate(flops=116_000_000_000, bytes_accessed=60_000_000, transcendentals=0),
-        )(v_loc.reshape(NU, 64, 2048), d_loc, z_loc.reshape(4, NU, 64, 512))
+        )(v_loc.reshape(NU, 64, 2048), t_loc.reshape(NU, 2, 64, 64), z_loc.reshape(4, NU, 64, 512))
         return out.reshape(4096, 512)
 
     return jax.shard_map(

time: 209 us -> 199 us (0.952)
  Pallas kernels: 198 us -> 191 us
  other arithmetic: 2.78 us -> 0 us
    pallas_call x1, Pallas kernels: 198 us -> 191 us  [local_apply(): pl.pallas_call(kernel, out_shape=jax.ShapeDtypeStruct((4, NU, 64, 512), F...]
where the time goes in v6:
time: 199 us
  Pallas kernels  191 us (96%)
  local copies, waits for them, and re-layouts  7.76 us (4%)
    pallas_call x1, Pallas kernels, local_apply(): pl.pallas_call(kernel, out_shape=jax.ShapeDtypeStruct((4, NU, 64, 512), F...  191 us
    unnamed x1, local copies, waits for them, and re-layouts  7.76 us

profile of v6, /device:TPU:0, one launch (start us, length us, event | category | flops | bytes accessed | tf_op | source)
XLA Modules:
  0.0 199.2 jit_solution(9826468057155638530)
XLA Ops:
  0.0 191.5 %shard_map.37 = f32[4,16,64,512]{3,2,1,0:T(8,128)} custom-call(f32[16,64,2048]{2,1,0:T(8,128)} %bitcast.5, f32[16,2,64,64]{3,2,1,0:T(8,128)} %bitcast.7, f32[4,16,64,512]{3,2,1,0:T(8,128)} %bitcast.6), custom_call_target="tpu_custom_call" | custom-call | flops 115999997952 | bytes 60000000 | tf_op jit(solution)/shard_map/pallas_call | solution.py:329
  191.5 7.8 %copy.5 = f32[4096,512]{1,0:T(8,128)} copy(f32[4096,512]{1,0:T(8,128)} %bitcast.4) | data formatting | bytes 16777216

commit v7 on v6

--- a/solution.py
+++ b/solution.py
@@ -16,6 +16,7 @@
 NP = NCH // 2
 LEAD, GROW, LEAD_MAX = (5, 3, 1), (4, 2, 8), (9, 5, 1)
 ZAHEAD = 4
+LAST = 2
 
 
 def split3(x):
@@ -51,7 +52,7 @@
 
 
 def kernel(
-    v_hbm, d_hbm, z_hbm, out_hbm,
+    v_hbm, d_hbm, z_hbm, x_hbm, v0_hbm, y_hbm,
     vbuf, xbuf, dbuf, vt3, vt3b, vn3, x3, x3b, y3, wacc, s1acc, s2acc, tmat,
     r1_sem, r2_sem, rp_sem, send_sem, z_sem, d_sem, o_sem,
 ):
@@ -173,7 +174,7 @@
         v = vbuf[c]
         store3(vn3, v)
         store3(vt, v.T)
-        g1 = dot(vt[1], vn3[1]) + dot(vt[0], vn3[0])
+        g1 = dot(vt[1, :192], vn3[1]) + dot(vt[0, :192], vn3[0])
         g2 = dot(vt[0], vn3[2]) + dot(vt[0], vn3[1])
         return g1, g2
 
@@ -193,7 +194,7 @@
         )
 
     def merge_1(s, s1, s2):
-        g = s1 + s2 + s2.T
+        g = s1 + s2[:192] + s2.T[:192]
         zero = jnp.zeros((64, 128), F32)
         d01, d23 = diag(s, 0), diag(s, 1)
         u01 = jnp.concatenate([jnp.where(low, 0.0, roll(g[:64, 128:])), zero], axis=0)
@@ -267,6 +268,19 @@
     first_g(1)
     finish(NU - 1, do_a(vt3b, x3b))
 
+    def x_copy(u):
+        return pltpu.make_async_copy(xbuf.at[u], x_hbm.at[:, u], o_sem.at[u])
+
+    def v_copy(u):
+        return pltpu.make_async_copy(vbuf.at[NCH - NU + u], v0_hbm.at[u], o_sem.at[NU + u])
+
+    def write_out(sa, lo, n):
+        @pl.when(sa == 0)
+        def _():
+            for u in range(n):
+                x_copy(lo + u).start()
+                v_copy(lo + u).start()
+
     def outer(k, carry):
         s = NU - k
         sa = s - 1
@@ -278,6 +292,7 @@
             c = off_a + i + 1
             carry = lax.cond(c % 2 == 0, lambda su: tick(c // 2, su), lambda su: su, carry)
             step(off_a + i, off_c + i, u)
+            write_out(sa, u - 1, 1)
             return carry
 
         def step2(j, carry):
@@ -285,6 +300,7 @@
             carry = tick((off_a + i + 2) // 2, carry)
             step(off_a + i, off_c + i, s + i)
             step(off_a + i + 1, off_c + i + 1, s + i + 1)
+            write_out(sa, s + i - 1, 2)
             return carry
 
         pairs = (k - 1) // 2
@@ -293,6 +309,12 @@
 
         carry = tick((off_a + k + 1) // 2, carry)
         next_z(sa)
+        write_out(sa, NU - 2, 1)
+
+        @pl.when(sa == 0)
+        def _():
+            v_copy(NU - 1).start()
+
         store3(x3b, do_c(off_c + k - 1, NU - 1))
         g1, g2 = do_g(off_a + k, vt3b)
         w = wacc[...] + do_a(vt3, x3)
@@ -306,16 +328,11 @@
 
     lax.fori_loop(1, NU, outer, carry)
 
-    def o_copy(u):
-        return pltpu.make_async_copy(xbuf.at[u], out_hbm.at[:, u], o_sem.at[u])
-
-    def final(u, _):
-        do_c(NCH - NU + u, u)
-        o_copy(u).start()
-        return 0
-
-    lax.fori_loop(0, NU, final, 0)
-    lax.fori_loop(0, NU, lambda u, _: (o_copy(u).wait(), 0)[1], 0)
+    y_copy = pltpu.make_async_copy(y3, y_hbm, o_sem.at[2 * NU])
+    y_copy.start()
+    x_copy(NU - 1).start()
+    lax.fori_loop(0, NU, lambda u, _: (x_copy(u).wait(), v_copy(u).wait(), 0)[2], 0)
+    y_copy.wait()
     sent = vbuf.at[:, pl.ds(0, 64), pl.ds(0, 128)]
     for k in range(3):
         remote(sent, sent, k, rp_sem.at[0], dev1).wait_send()
@@ -323,14 +340,24 @@
     remote(sent, sent, 3, rp_sem.at[0], devp).wait_send()
 
 
+def last_update(x_ref, v_ref, y_ref, out_ref):
+    for i in range(LAST):
+        upd = mm6(split3(v_ref[i]), (y_ref[0], y_ref[1], y_ref[2]))
+        out_ref[:, i] = x_ref[:, i] - upd.reshape(4, 64, 512)
+
+
 def solution(mesh):
     def local_apply(v_loc, t_loc, z_loc):
         dma = pltpu.SemaphoreType.DMA
-        out = pl.pallas_call(
+        x, v0, y = pl.pallas_call(
             kernel,
-            out_shape=jax.ShapeDtypeStruct((4, NU, 64, 512), F32),
+            out_shape=(
+                jax.ShapeDtypeStruct((4, NU, 64, 512), F32),
+                jax.ShapeDtypeStruct((NU, 256, 256), F32),
+                jax.ShapeDtypeStruct((3, 256, 512), BF16),
+            ),
             in_specs=[pl.BlockSpec(memory_space=pl.ANY)] * 3,
-            out_specs=pl.BlockSpec(memory_space=pl.ANY),
+            out_specs=(pl.BlockSpec(memory_space=pl.ANY),) * 3,
             scratch_shapes=[
                 pltpu.VMEM((NCH, 256, 256), F32),
                 pltpu.VMEM((NU, 4, 64, 512), F32),
@@ -342,17 +369,33 @@
                 pltpu.VMEM((3, 256, 512), BF16),
                 pltpu.VMEM((3, 256, 512), BF16),
                 pltpu.VMEM((256, 512), F32),
-                pltpu.VMEM((256, 256), F32),
+                pltpu.VMEM((192, 256), F32),
                 pltpu.VMEM((256, 256), F32),
                 pltpu.VMEM((256, 256), F32),
                 dma((NP,)), dma((NP,)), dma((NP,)),
-                dma((4,)), dma((NU,)), dma((3,)), dma((NU,)),
+                dma((4,)), dma((NU,)), dma((3,)), dma((2 * NU + 1,)),
             ],
             compiler_params=pltpu.CompilerParams(
                 collective_id=0, has_side_effects=True, vmem_limit_bytes=67_043_328
             ),
             cost_estimate=pl.CostEstimate(flops=116_000_000_000, bytes_accessed=60_000_000, transcendentals=0),
         )(v_loc.reshape(NU, 64, 2048), t_loc.reshape(NU, 2, 64, 64), z_loc.reshape(4, NU, 64, 512))
+        x_spec = pl.BlockSpec((4, LAST, 64, 512), lambda i: (0, i, 0, 0))
+        out = pl.pallas_call(
+            last_update,
+            out_shape=jax.ShapeDtypeStruct((4, NU, 64, 512), F32),
+            grid=(NU // LAST,),
+            in_specs=[
+                x_spec,
+                pl.BlockSpec((LAST, 256, 256), lambda i: (i, 0, 0)),
+                pl.BlockSpec((3, 256, 512), lambda i: (0, 0, 0)),
+            ],
+            out_specs=x_spec,
+            compiler_params=pltpu.CompilerParams(
+                dimension_semantics=("arbitrary",), vmem_limit_bytes=67_043_328
+            ),
+            cost_estimate=pl.CostEstimate(flops=6_500_000_000, bytes_accessed=22_000_000, transcendentals=0),
+        )(x, v0, y)
         return out.reshape(4096, 512)
 
     return jax.shard_map(

time: 199 us -> 191 us (0.960)
  local copies, waits for them, and re-layouts: 7.76 us -> 0 us
    unnamed x1 -> x0, local copies, waits for them, and re-layouts: 7.76 us -> none
    pallas_call x1 -> x2, Pallas kernels: 191 us -> 191 us  [the longest x1 178 us: local_apply(): pl.pallas_call(kernel, out_shape=(jax.ShapeDtypeStruct((4, NU, 64, 512),...]
where the time goes in v7:
time: 191 us
  Pallas kernels  191 us (100%)
    pallas_call x1, Pallas kernels, local_apply(): pl.pallas_call(kernel, out_shape=(jax.ShapeDtypeStruct((4, NU, 64, 512),...  178 us
    pallas_call x1, Pallas kernels, local_apply(): pl.pallas_call(last_update, out_shape=jax.ShapeDtypeStruct((4, NU, 64, 51...  13.2 us

profile of v7, /device:TPU:0, one launch (start us, length us, event | category | flops | bytes accessed | tf_op | source)
XLA Modules:
  0.0 191.0 jit_solution(2856476163224223201)
XLA Ops:
  0.0 177.8 %shard_map.37 = (f32[4,16,64,512]{3,2,1,0:T(8,128)}, f32[16,256,256]{2,1,0:T(8,128)}, bf16[3,256,512]{2,1,0:T(8,128)(2,1)}) custom-call(f32[16,64,2048]{2,1,0:T(8,128)} %bitcast.4, f32[16,2,64,64]{3,2,1,0:T(8,128)} %bitcast.6, f32[4,16,64,512]{3,2,1,0:T(8,128)} %bitcast.5), custom_call_target="tpu_custom_call" | custom-call | flops 115999997952 | bytes 60000000 | tf_op jit(solution)/shard_map/pallas_call | solution.py:352
  177.8 13.2 %shard_map.38 = f32[4,16,64,512]{3,2,1,0:T(8,128)} custom-call(f32[4,16,64,512]{3,2,1,0:T(8,128)} %get-tuple-element.8.x_ref, f32[16,256,256]{2,1,0:T(8,128)} %get-tuple-element.9.v_ref, bf16[3,256,512]{2,1,0:T(8,128)(2,1)} %get-tuple-element.10.y_ref), custom_call_target="tpu_custom_call" | custom-call | flops 6499999744 | bytes 22000000 | tf_op jit(solution)/shard_map/pallas_call | solution.py:384

commit v8 on v7

--- a/solution.py
+++ b/solution.py
@@ -14,7 +14,7 @@
 NU = 16
 NCH = NU * (NU + 1) // 2
 NP = NCH // 2
-LEAD, GROW, LEAD_MAX = (5, 3, 1), (4, 2, 8), (9, 5, 1)
+LEAD = (7, 4, 1)
 ZAHEAD = 4
 LAST = 2
 
@@ -97,39 +97,33 @@
         x = vbuf.at[pl.ds(2 * p, 2), :, pl.ds(pl.multiple_of((1 - q) * 128, 128), 128)]
         remote(x, x, 3, rp_sem.at[p], devp).wait_recv()
 
-    def target(i, p):
-        ahead = jnp.minimum(LEAD[i] + p * GROW[i] // 16, LEAD_MAX[i])
-        return jnp.minimum(p + ahead, NP)
-
-    def run0(lo, hi, su):
-        def body(p, su):
-            s, u = su
-            for i in range(2):
+    def send_own(p, su):
+        s, u = su
+        for i in range(2):
+
+            @pl.when(p < NP)
+            def _():
                 stage0(p, 2 * p + i, s, u)
-                last = u == NU - 1
-                s2 = jnp.where(last, jnp.maximum(s - 1, 0), s)
-                s, u = s2, jnp.where(last, s2, u + 1)
-            return s, u
-
-        return lax.fori_loop(lo, hi, body, su)
-
-    def run(i, lo, hi):
-        def body(n, _):
-            (None, stage1, stage2)[i](n)
-            return 0
-
-        lax.fori_loop(lo, hi, body, 0)
+
+            last = u == NU - 1
+            s2 = jnp.where(last, jnp.maximum(s - 1, 0), s)
+            s, u = s2, jnp.where(last, s2, u + 1)
+        return s, u
 
     def tick(p, su):
-        for i in (1, 2):
-            run(i, target(i, p), target(i, p + 1))
-        su = run0(target(0, p), target(0, p + 1), su)
+        @pl.when(p + LEAD[1] < NP)
+        def _():
+            stage1(p + LEAD[1])
+
+        @pl.when(p + LEAD[2] < NP)
+        def _():
+            stage2(p + LEAD[2])
 
         @pl.when(p < NP)
         def _():
             stage3(p)
 
-        return su
+        return send_own(p + LEAD[0], su)
 
     barrier = pltpu.get_barrier_semaphore()
     for dev in (dev1, dev2, devp):
@@ -150,9 +144,9 @@
 
     for i in range(ZAHEAD):
         z_copy(NU - 1 - i).start()
-    carry = run0(0, target(0, 0), (jnp.int32(NU - 1), jnp.int32(NU - 1)))
-    for i in (1, 2):
-        run(i, 0, target(i, 0))
+    carry = lax.fori_loop(0, LEAD[0], send_own, (jnp.int32(NU - 1), jnp.int32(NU - 1)))
+    lax.fori_loop(0, LEAD[1], lambda p, _: (stage1(p), 0)[1], 0)
+    lax.fori_loop(0, LEAD[2], lambda p, _: (stage2(p), 0)[1], 0)
     d_send.wait()
     d_loc.wait()
 
@@ -340,10 +334,35 @@
     remote(sent, sent, 3, rp_sem.at[0], devp).wait_send()
 
 
-def last_update(x_ref, v_ref, y_ref, out_ref):
-    for i in range(LAST):
-        upd = mm6(split3(v_ref[i]), (y_ref[0], y_ref[1], y_ref[2]))
-        out_ref[:, i] = x_ref[:, i] - upd.reshape(4, 64, 512)
+def last_update(x_hbm, v_hbm, y_hbm, out_hbm, xb, vb, yb, sem):
+    def x_in(u):
+        return pltpu.make_async_copy(x_hbm.at[:, u], xb.at[u], sem.at[u])
+
+    def v_in(u):
+        return pltpu.make_async_copy(v_hbm.at[u], vb.at[u], sem.at[NU + u])
+
+    def x_out(u):
+        return pltpu.make_async_copy(xb.at[u], out_hbm.at[:, u], sem.at[2 * NU + u])
+
+    y_in = pltpu.make_async_copy(y_hbm, yb, sem.at[3 * NU])
+    y_in.start()
+    lax.fori_loop(0, NU, lambda u, _: (v_in(u).start(), x_in(u).start(), 0)[2], 0)
+    y_in.wait()
+
+    def body(j, _):
+        for i in range(LAST):
+            x_in(LAST * j + i).wait()
+            v_in(LAST * j + i).wait()
+        for i in range(LAST):
+            u = LAST * j + i
+            upd = mm6(split3(vb[u]), (yb[0], yb[1], yb[2]))
+            xb[u] = xb[u] - upd.reshape(4, 64, 512)
+        for i in range(LAST):
+            x_out(LAST * j + i).start()
+        return 0
+
+    lax.fori_loop(0, NU // LAST, body, 0)
+    lax.fori_loop(0, NU, lambda u, _: (x_out(u).wait(), 0)[1], 0)
 
 
 def solution(mesh):
@@ -380,20 +399,18 @@
             ),
             cost_estimate=pl.CostEstimate(flops=116_000_000_000, bytes_accessed=60_000_000, transcendentals=0),
         )(v_loc.reshape(NU, 64, 2048), t_loc.reshape(NU, 2, 64, 64), z_loc.reshape(4, NU, 64, 512))
-        x_spec = pl.BlockSpec((4, LAST, 64, 512), lambda i: (0, i, 0, 0))
         out = pl.pallas_call(
             last_update,
             out_shape=jax.ShapeDtypeStruct((4, NU, 64, 512), F32),
-            grid=(NU // LAST,),
-            in_specs=[
-                x_spec,
-                pl.BlockSpec((LAST, 256, 256), lambda i: (i, 0, 0)),
-                pl.BlockSpec((3, 256, 512), lambda i: (0, 0, 0)),
+            in_specs=[pl.BlockSpec(memory_space=pl.ANY)] * 3,
+            out_specs=pl.BlockSpec(memory_space=pl.ANY),
+            scratch_shapes=[
+                pltpu.VMEM((NU, 4, 64, 512), F32),
+                pltpu.VMEM((NU, 256, 256), F32),
+                pltpu.VMEM((3, 256, 512), BF16),
+                dma((3 * NU + 1,)),
             ],
-            out_specs=x_spec,
-            compiler_params=pltpu.CompilerParams(
-                dimension_semantics=("arbitrary",), vmem_limit_bytes=67_043_328
-            ),
+            compiler_params=pltpu.CompilerParams(vmem_limit_bytes=67_043_328),
             cost_estimate=pl.CostEstimate(flops=6_500_000_000, bytes_accessed=22_000_000, transcendentals=0),
         )(x, v0, y)
         return out.reshape(4096, 512)

time: 191 us -> 188 us (0.984)
  Pallas kernels: 191 us -> 188 us
    pallas_call x1, Pallas kernels: 13.2 us -> 10.9 us  [local_apply(): pl.pallas_call(last_update, out_shape=jax.ShapeDtypeStruct((4, NU, 64, 51...]
where the time goes in v8:
time: 188 us
  Pallas kernels  188 us (100%)
    pallas_call x1, Pallas kernels, local_apply(): pl.pallas_call(kernel, out_shape=(jax.ShapeDtypeStruct((4, NU, 64, 512),...  177 us
    pallas_call x1, Pallas kernels, local_apply(): pl.pallas_call(last_update, out_shape=jax.ShapeDtypeStruct((4, NU, 64, 51...  10.9 us

profile of v8, /device:TPU:0, one launch (start us, length us, event | category | flops | bytes accessed | tf_op | source)
XLA Modules:
  0.0 187.7 jit_solution(1023931103583326347)
XLA Ops:
  0.0 176.8 %shard_map.37 = (f32[4,16,64,512]{3,2,1,0:T(8,128)}, f32[16,256,256]{2,1,0:T(8,128)}, bf16[3,256,512]{2,1,0:T(8,128)(2,1)}) custom-call(f32[16,64,2048]{2,1,0:T(8,128)} %bitcast.4, f32[16,2,64,64]{3,2,1,0:T(8,128)} %bitcast.6, f32[4,16,64,512]{3,2,1,0:T(8,128)} %bitcast.5), custom_call_target="tpu_custom_call" | custom-call | flops 115999997952 | bytes 60000000 | tf_op jit(solution)/shard_map/pallas_call | solution.py:371
  176.8 10.9 %shard_map.38 = f32[4,16,64,512]{3,2,1,0:T(8,128)} custom-call(f32[4,16,64,512]{3,2,1,0:T(8,128)} %get-tuple-element.8.x_hbm, f32[16,256,256]{2,1,0:T(8,128)} %get-tuple-element.9.v_hbm, bf16[3,256,512]{2,1,0:T(8,128)(2,1)} %get-tuple-element.10.y_hbm), custom_call_target="tpu_custom_call" | custom-call | flops 6499999744 | bytes 22000000 | tf_op jit(solution)/shard_map/pallas_call | solution.py:402

commit v9 on v8

--- a/solution.py
+++ b/solution.py
@@ -15,6 +15,7 @@
 NCH = NU * (NU + 1) // 2
 NP = NCH // 2
 LEAD = (7, 4, 1)
+PROLOGUE = (0, 0, 0, 0, 1, 0, 1, 1, 0, 0, 1, 0, 2, 2), (1,)
 ZAHEAD = 4
 LAST = 2
 
@@ -110,7 +111,7 @@
             s, u = s2, jnp.where(last, s2, u + 1)
         return s, u
 
-    def tick(p, su):
+    def tick(p):
         @pl.when(p + LEAD[1] < NP)
         def _():
             stage1(p + LEAD[1])
@@ -122,8 +123,6 @@
         @pl.when(p < NP)
         def _():
             stage3(p)
-
-        return send_own(p + LEAD[0], su)
 
     barrier = pltpu.get_barrier_semaphore()
     for dev in (dev1, dev2, devp):
@@ -144,9 +143,20 @@
 
     for i in range(ZAHEAD):
         z_copy(NU - 1 - i).start()
-    carry = lax.fori_loop(0, LEAD[0], send_own, (jnp.int32(NU - 1), jnp.int32(NU - 1)))
-    lax.fori_loop(0, LEAD[1], lambda p, _: (stage1(p), 0)[1], 0)
-    lax.fori_loop(0, LEAD[2], lambda p, _: (stage2(p), 0)[1], 0)
+    chunks = [(s, u) for s in range(NU - 1, -1, -1) for u in range(s, NU)]
+    done = [0, 0, 0]
+
+    def prologue(stages):
+        for i in stages:
+            p = done[i]
+            done[i] += 1
+            if i == 0:
+                stage0(p, 2 * p, *chunks[2 * p])
+                stage0(p, 2 * p + 1, *chunks[2 * p + 1])
+            else:
+                (stage1 if i == 1 else stage2)(p)
+
+    prologue(PROLOGUE[0])
     d_send.wait()
     d_loc.wait()
 
@@ -224,7 +234,7 @@
     def offset(s):
         return (NU - 1 - s) * (NU - s) // 2
 
-    carry = tick(0, carry)
+    stage3(0)
     z_copy(NU - 1).wait()
     wacc[...] = jnp.zeros_like(wacc)
     s1acc[...], s2acc[...] = do_g(0, vt3)
@@ -262,6 +272,9 @@
     first_g(1)
     finish(NU - 1, do_a(vt3b, x3b))
 
+    prologue(PROLOGUE[1])
+    carry = tuple(jnp.int32(i) for i in chunks[2 * done[0]])
+
     def x_copy(u):
         return pltpu.make_async_copy(xbuf.at[u], x_hbm.at[:, u], o_sem.at[u])
 
@@ -284,14 +297,21 @@
         def step1(u, carry):
             i = u - s
             c = off_a + i + 1
-            carry = lax.cond(c % 2 == 0, lambda su: tick(c // 2, su), lambda su: su, carry)
+
+            def tick_and_send(su):
+                tick(c // 2)
+                return send_own(c // 2 + LEAD[0], su)
+
+            carry = lax.cond(c % 2 == 0, tick_and_send, lambda su: su, carry)
             step(off_a + i, off_c + i, u)
             write_out(sa, u - 1, 1)
             return carry
 
         def step2(j, carry):
             i = 2 * j
-            carry = tick((off_a + i + 2) // 2, carry)
+            p = (off_a + i + 2) // 2
+            tick(p)
+            carry = send_own(p + LEAD[0], carry)
             step(off_a + i, off_c + i, s + i)
             step(off_a + i + 1, off_c + i + 1, s + i + 1)
             write_out(sa, s + i - 1, 2)
@@ -301,7 +321,9 @@
         carry = lax.fori_loop(0, pairs, step2, carry)
         carry = lax.fori_loop(s + 2 * pairs, NU - 1, step1, carry)
 
-        carry = tick((off_a + k + 1) // 2, carry)
+        p = (off_a + k + 1) // 2
+        tick(p)
+        carry = send_own(p + LEAD[0], carry)
         next_z(sa)
         write_out(sa, NU - 2, 1)
 

time: 188 us -> 187 us (level)
  no operation moved by 1% of the time
where the time goes in v9:
time: 187 us
  Pallas kernels  187 us (100%)
    pallas_call x1, Pallas kernels, local_apply(): pl.pallas_call(kernel, out_shape=(jax.ShapeDtypeStruct((4, NU, 64, 512),...  176 us
    pallas_call x1, Pallas kernels, local_apply(): pl.pallas_call(last_update, out_shape=jax.ShapeDtypeStruct((4, NU, 64, 51...  10.9 us

profile of v9, /device:TPU:0, one launch (start us, length us, event | category | flops | bytes accessed | tf_op | source)
XLA Modules:
  0.0 186.5 jit_solution(3993292301773990099)
XLA Ops:
  0.0 175.6 %shard_map.37 = (f32[4,16,64,512]{3,2,1,0:T(8,128)}, f32[16,256,256]{2,1,0:T(8,128)}, bf16[3,256,512]{2,1,0:T(8,128)(2,1)}) custom-call(f32[16,64,2048]{2,1,0:T(8,128)} %bitcast.4, f32[16,2,64,64]{3,2,1,0:T(8,128)} %bitcast.6, f32[4,16,64,512]{3,2,1,0:T(8,128)} %bitcast.5), custom_call_target="tpu_custom_call" | custom-call | flops 115999997952 | bytes 60000000 | tf_op jit(solution)/shard_map/pallas_call | solution.py:393
  175.6 10.9 %shard_map.38 = f32[4,16,64,512]{3,2,1,0:T(8,128)} custom-call(f32[4,16,64,512]{3,2,1,0:T(8,128)} %get-tuple-element.8.x_hbm, f32[16,256,256]{2,1,0:T(8,128)} %get-tuple-element.9.v_hbm, bf16[3,256,512]{2,1,0:T(8,128)(2,1)} %get-tuple-element.10.y_hbm), custom_call_target="tpu_custom_call" | custom-call | flops 6499999744 | bytes 22000000 | tf_op jit(solution)/shard_map/pallas_call | solution.py:424
